TPU v7x, 128 devices: a whole 4x4x4 slice. The times are simulated.
128 devices in a mesh: chan: 8 (over x, core), vox: 16 (over z, y).
Axes of the slice: x: 4, y: 4, z: 4, core: 2. Of those that a mesh axis runs over, the one named last changes fastest.
Arguments:
- features: bfloat16 [512, 5632], P('chan'), may hold values from -6 to 6
- hrf_filters: float32 [3, 5632, 16], P(None, 'chan'), may hold values from -1.5 to 1.5
- weights: bfloat16 [3, 5632, 81920], P(None, 'chan', 'vox'), may hold values from -0.046875 to 0.046875
- voxel_parcel: int32 [81920], P('vox'), may hold values from 0 to 1599, as said below
- parcel_owner: int32 [1600], replicated, may hold values from 0 to 15, as said below
Outputs:
- owned: bfloat16 [256, 640, 512], P('vox', None, 'chan')
Inputs may be any that keep to these rules, and one draw needn't show every extreme that they name: `voxel_parcel`: among the 5120 voxels of one index of vox, at most 640 belong to parcels of one owner, and some owner gets exactly 640; one owner gets exactly 640 from every index of vox. `parcel_owner`: every owner holds exactly 100 parcels.
All inputs are finite; a program needn't handle non-finite values.
Results may differ from a plain program's by a relative error of at most 0.01.
Values may be sent and summed in bfloat16 or wider, within the bound.
A program may use at most 128 MiB of HBM per device.

v0:
```python
import jax
import jax.numpy as jnp
from jax import lax
from jax.sharding import PartitionSpec as P

FILTER_TAPS = 16
TAP_SPACING = 2


def shards(features, hrf_filters, weights, voxel_parcel, parcel_owner):
    by_channel = lax.all_to_all(features, "chan", split_axis=1, concat_axis=0, tiled=True)
    series = by_channel.astype(jnp.float32).T
    time_len = series.shape[1]
    chan_width = series.shape[0]
    largest_delay = TAP_SPACING * (FILTER_TAPS - 1)
    padded = jnp.pad(series, ((0, 0), (largest_delay, 0)))
    filtered = jnp.zeros((hrf_filters.shape[0], chan_width, time_len), jnp.float32)
    for delay_index in range(FILTER_TAPS):
        window_start = largest_delay - TAP_SPACING * delay_index
        lagged = padded[:, window_start : window_start + time_len]
        filtered = filtered + hrf_filters[:, :, delay_index][:, :, None] * lagged[None]
    design = filtered.astype(jnp.bfloat16).reshape(-1, time_len)
    weight_panel = weights.reshape(-1, weights.shape[2])
    partial_value = lax.dot_general(
        weight_panel, design, (((0,), (0,)), ((), ())), preferred_element_type=jnp.float32
    )
    owner_count = lax.axis_size("vox")
    chan_count = lax.axis_size("chan")
    block_len = time_len // chan_count
    send_cap = 2 * voxel_parcel.shape[0] // owner_count
    owners_here = jnp.take(parcel_owner, voxel_parcel)
    onehot = (owners_here[:, None] == jnp.arange(owner_count, dtype=jnp.int32)[None, :]).astype(
        jnp.int32
    )
    before = jnp.cumsum(onehot, axis=0) - onehot
    slot_index = jnp.sum(before * onehot, axis=1)
    target_row = owners_here * send_cap + slot_index
    rounded = partial_value.astype(jnp.bfloat16)
    packed = jnp.zeros((owner_count * send_cap, time_len), jnp.bfloat16).at[target_row].set(rounded)
    packed = packed.reshape(owner_count, send_cap, time_len)
    received = lax.all_to_all(
        lax.all_to_all(packed, "chan", split_axis=2, concat_axis=2, tiled=True),
        "vox",
        split_axis=0,
        concat_axis=0,
        tiled=True,
    )
    summed = (
        received.astype(jnp.float32)
        .reshape(owner_count, send_cap, chan_count, block_len)
        .sum(axis=2)
    )
    return summed.astype(jnp.bfloat16)


def solution(mesh):
    return jax.shard_map(
        shards,
        mesh=mesh,
        in_specs=(P("chan", None), P(None, "chan", None), P(None, "chan", "vox"), P("vox"), P()),
        out_specs=P("vox", None, "chan"),
        check_vma=False,
    )
```

profile of v0, /device:TPU:0, one launch (start us, length us, event | category | flops | bytes accessed | tf_op | source)
XLA Modules:
  0.0 451.6 jit_solution(16848935278900701156)
XLA Ops:
  0.0 0.0 copy-start
  0.0 1.9 all_to_all.16
  1.9 0.0 copy-start.2
  1.9 0.0 copy-start.3
  1.9 1.0 copy.26
  2.9 4.4 all-to-all-start
  7.3 0.0 copy-done.2
  7.3 0.1 fusion.40
  7.4 0.0 copy-done.3
  7.4 0.0 copy-done
  7.4 28.7 %gather_fusion = s32[5120]{0:T(1024)S(1)} fusion(s32[1600]{0:T(1024)S(1)} %copy-done, s32[5120]{0:T(1024)S(1)} %fusion.39), kind=kCustom, calls=%fused_computation | custom fusion | bytes 61440 | tf_op jit(solution)/shard_map/jit(_take)/gather | solution.py:31
  36.2 4.7 %reduce-window.6 = s32[16,40,128]{2,1,0:T(8,128)S(1)} reduce-window(s32[16,40,128]{2,1,0:T(8,128)S(1)} %fusion.38, s32[]{:T(128)} %constant.11.clone.1), window={size=1x1x128 pad=0_0x0_0x127_0}, to_apply=%region_0.1 | reduce-window | flops 10403840 | bytes 655364 | tf_op jit(solution)/shard_map/reduce-window
  40.8 0.5 slice_reduce_fusion
  41.3 0.2 reduce-window.9
  41.5 0.2 broadcast_add_fusion
  41.7 0.1 fusion.37
  41.9 0.0 all-to-all-done
  42.0 0.1 transpose.61
  42.1 8.1 %pad_slice_fusion.14 = (f32[704,512]{0,1:T(8,128)}, f32[704,512]{0,1:T(8,128)}, f32[704,512]{0,1:T(8,128)}, f32[704,512]{0,1:T(8,128)}, f32[704,512]{0,1:T(8,128...) fusion(f32[704,512]{0,1:T(8,128)S(1)} %bitcast.67), kind=kLoop, calls=%fused_computation.53 | loop fusion | bytes 23068672 | tf_op jit(solution)/shard_map/slice | solution.py:20
  50.2 0.4 copy.27
  50.6 1.9 copy.28
  52.5 3.0 copy.29
  55.5 3.0 copy.30
  58.5 3.0 copy.31
  61.4 3.0 copy.32
  64.4 3.0 copy.33
  67.4 3.0 copy.34
  70.3 3.0 copy.35
  73.4 2.9 copy.36
  76.3 3.0 copy.37
  79.3 3.0 copy.38
  82.3 3.0 copy.39
  85.3 3.0 copy.40
  88.3 3.0 copy.41
  91.3 3.0 copy.42
  94.3 34.5 %fusion = bf16[5120,512]{0,1:T(8,128)(2,1)} fusion(bf16[3,704,5120]{2,1,0:T(8,128)(2,1)} %param.7, f32[704,512]{1,0:T(8,128)} %copy.42, f32[3,704]{1,0:T(4,128)S(1)} %get-tuple-element.36, f32[704,512]{1,0:T(8,128)} %copy.41, f32[3,704]{1,0:T(4,128)S(1)} %get-tuple-element.37, f32[704,512]{1,0:T(8,128)} %copy.40, f32[3,704]{1,0:T(4,128)S(1)} %get-tuple-element.38, ...), kind=kOutput, calls=%fused_computation.3 | convolution fusion | flops 11110187008 | bytes 50073600 | tf_op jit(solution)/shard_map/dot_general | solution.py:24
  128.9 8.0 %copy.43 = bf16[5120,512]{1,0:T(8,128)(2,1)} copy(bf16[5120,512]{0,1:T(8,128)(2,1)} %fusion) | data formatting | bytes 10485760 | tf_op jit(solution)/shard_map/convert_element_type | solution.py:38
  136.8 29.0 %scatter_custom_fusion = bf16[10240,512]{1,0:T(8,128)(2,1)} fusion(s32[5120]{0:T(1024)S(1)} %compare_select_fusion, bf16[5120,512]{1,0:T(8,128)(2,1)} %copy.43, bf16[]{:T(256)} %constant.10.clone.1), kind=kCustom, calls=%fused_computation.4 | custom fusion | bytes 10486272 | tf_op jit(solution)/shard_map/scatter | solution.py:39
  165.8 17.6 %copy.44 = bf16[16,640,512]{1,0,2:T(8,128)(2,1)} copy(bf16[16,640,512]{2,1,0:T(8,128)(2,1)} %bitcast.65) | data formatting | bytes 20971520 | tf_op jit(solution)/shard_map/reshape | solution.py:40
  183.4 124.9 %all_to_all.23 = bf16[16,640,512]{1,0,2:T(8,128)(2,1)} all-to-all(bf16[16,640,512]{1,0,2:T(8,128)(2,1)} %copy.44), channel_id=1, replica_groups=mesh['chan'=8,'vox'=16] {'chan'}, dimensions={2} | all-to-all | bytes 20971520 | tf_op jit(solution)/shard_map/all_to_all | solution.py:42
  308.3 10.2 %copy.45 = bf16[16,640,512]{1,2,0:T(8,128)(2,1)} copy(bf16[16,640,512]{1,0,2:T(8,128)(2,1)} %all_to_all.23) | data formatting | bytes 20971520 | tf_op jit(solution)/shard_map/all_to_all | solution.py:42
  318.5 126.1 %all_to_all.24 = bf16[16,640,512]{1,2,0:T(8,128)(2,1)} all-to-all(bf16[16,640,512]{1,2,0:T(8,128)(2,1)} %copy.45), channel_id=1, replica_groups=mesh['chan'=8,'vox'=16] {'vox'}, dimensions={0} | all-to-all | bytes 20971520 | tf_op jit(solution)/shard_map/all_to_all | solution.py:41
  444.5 0.0 copy-start.1
  444.5 7.1 %reduce = bf16[16,640,64]{1,2,0:T(8,128)(2,1)} reduce(bf16[16,640,8,64]{1,3,2,0:T(8,128)(2,1)} %bitcast.66, bf16[]{:T(256)} %constant.10.clone.1), dimensions={2}, to_apply=%region_4.5.clone | reduce | flops 4587520 | bytes 11796482 | tf_op jit(solution)/shard_map/reduce_sum | solution.py:51
  451.6 0.0 copy-done.1
  (12 shorter events, 0.1 us)
Async XLA Ops:
  0.0 7.4 %copy-start = (s32[1600]{0:T(1024)S(1)}, s32[1600]{0:T(1024)}, u32[]{:S(2)}) copy-start(s32[1600]{0:T(1024)} %param.9) | copy-start | bytes 19204
  1.9 5.4 %copy-start.2 = (f32[3,704,16]{1,2,0:T(8,128)S(1)}, f32[3,704,16]{1,2,0:T(8,128)}, u32[]{:S(2)}) copy-start(f32[3,704,16]{1,2,0:T(8,128)} %param.6) | copy-start | bytes 405508
  1.9 5.5 %copy-start.3 = (s32[5120]{0:T(1024)S(1)}, s32[5120]{0:T(1024)}, u32[]{:S(2)}) copy-start(s32[5120]{0:T(1024)} %param.8) | copy-start | bytes 61444
  2.9 39.0 %all-to-all-start = ((bf16[64,8,704]{2,0,1:T(8,128)(2,1)}), bf16[64,8,704]{2,0,1:T(8,128)(2,1)S(1)}, u32[]{:S(2)}, u32[]{:S(2)}) async-start(bf16[64,8,704]{2,0,1:T(8,128)(2,1)} %copy.26), calls=%async_computation | async-start | bytes 1572864 | tf_op jit(solution)/shard_map/all_to_all | solution.py:11
  444.5 7.1 %copy-start.1 = (s32[1600]{0:T(1024)S(1)}, s32[1600]{0:T(1024)}, u32[]{:S(2)}) copy-start(s32[1600]{0:T(1024)} %param.9) | copy-start | bytes 19204
where the time goes:
time: 453 us; the launch traced here: 452 us
  blocking collectives  251 us (55%)
  local copies, waits for them, and re-layouts  149 us (33%)
  matrix products  34.5 us (8%)
  other arithmetic  12.4 us (3%)
    all_to_all x1, blocking collectives, shards(): lax.all_to_all(lax.all_to_all(packed, 'chan', split_axis=2, concat_axis=2...  126 us
    all_to_all x1, blocking collectives, shards(): lax.all_to_all(packed, 'chan', split_axis=2, concat_axis=2, tiled=True)  125 us
    slice x16, local copies, waits for them, and re-layouts, shards(): lagged = padded[:, window_start:window_start + time_len]  51.8 us
    dot_general x1, matrix products, shards(): lax.dot_general(weight_panel, design, (((0,), (0,)), ((), ())), preferred...  34.5 us
    scatter x1, local copies, waits for them, and re-layouts, shards(): jnp.zeros((owner_count * send_cap, time_len), jnp.bfloat16).at[target_row]  29 us
    gather x1, local copies, waits for them, and re-layouts, shards(): owners_here = jnp.take(parcel_owner, voxel_parcel)  28.7 us
    reshape x1, local copies, waits for them, and re-layouts, shards(): packed = packed.reshape(owner_count, send_cap, time_len)  17.6 us
    all_to_all x1, local copies, waits for them, and re-layouts, shards(): lax.all_to_all(packed, 'chan', split_axis=2, concat_axis=2, tiled=True)  10.2 us
  transfers between devices with their start and end apart: 1, of which 0 were waited for; matrix products, arithmetic and copies ran while one was open for 8% of the time, Pallas kernels for 0%

commit v1 on v0

v1 whole, which is shorter than its diff:
```python
import functools

import jax
import jax.numpy as jnp
from jax import lax
from jax.experimental import pallas as pl
from jax.experimental.pallas import tpu as pltpu
from jax.sharding import PartitionSpec as P

MESH = pl.DeviceIdType.MESH
TAP_SPACING = 2
VMEM_LIMIT = 66_000_000
LANES = 128
SLAB = 512
SORT = 256
TILE = 8
LOCAL_TILES = 60
GROUP = 12
LAG = 2


def up(value, multiple):
    return -(-value // multiple) * multiple


def main_kernel(
    sizes,
    feat_ref, hrf_ref, w_ref, out_ref,
    wv, fe, series, coef, design, own, dsend, drecv, rsend, rrecv,
    w_sem, f_local, f_send, f_recv, d_send, d_recv, r_send, r_recv,
):
    n_chan, bases, taps, width, wide, block, steps = sizes
    pairs = n_chan // 2
    half = SLAB // 2
    me = lax.axis_index("chan")
    chip = me // 2
    core = me % 2
    partner = chip * 2 + (1 - core)
    right = lax.rem(chip + 1, pairs) * 2 + core
    left = lax.rem(chip + pairs - 1, pairs) * 2 + core
    shift = core * (wide - width)

    def weight_copy(i):
        cols = pl.ds(pl.multiple_of(i * SLAB, SLAB), SLAB)
        rows = pl.ds(pl.multiple_of(shift, 64), width)
        return pltpu.make_async_copy(w_ref.at[:, :, cols], wv.at[:, rows, cols], w_sem.at[i])

    def window(k):
        start = k * width - lax.rem(k, 2) * (wide - width)
        return pl.ds(pl.multiple_of(start, LANES), wide)

    local = pltpu.make_async_copy(feat_ref.at[:, window(me)], fe.at[me], f_local)
    local.start()

    barrier = pltpu.get_barrier_semaphore()
    for d in range(1, n_chan):
        pl.semaphore_signal(
            barrier, inc=1, device_id={"chan": lax.rem(me + d, n_chan)}, device_id_type=MESH
        )
    pl.semaphore_wait(barrier, n_chan - 1)

    def feature_copy(d):
        peer = lax.rem(me + d, n_chan)
        return pltpu.make_async_remote_copy(
            src_ref=feat_ref.at[:, window(peer)],
            dst_ref=fe.at[me],
            send_sem=f_send.at[d - 1],
            recv_sem=f_recv.at[d - 1],
            device_id={"chan": peer},
            device_id_type=MESH,
        )

    for d in (4, 3, 5, 2, 6, 1, 7):
        if d < n_chan:
            feature_copy(d).start()

    @pl.loop(0, steps)
    def _(i):
        weight_copy(i).start()

    blank = pl.ds(pl.multiple_of((1 - core) * width, 64), wide - width)
    for b in range(bases):
        wv[b, blank, :] = jnp.zeros((wide - width, wv.shape[2]), wv.dtype)
    coef[...] = jnp.zeros(coef.shape, coef.dtype)

    @pl.when(core == 0)
    def _():
        coef[:, :, :width] = hrf_ref[...]

    @pl.when(core == 1)
    def _():
        coef[:, :, wide - width :] = hrf_ref[...]

    pad = 32
    series[:pad, :] = jnp.zeros((pad, wide), jnp.float32)
    local.wait()
    for d in range(1, n_chan):
        feature_copy(d).wait_recv()

    @pl.loop(0, n_chan)
    def _(r):
        rows = pl.ds(pl.multiple_of(pad + r * block, 32), block)
        series[rows, :] = fe[r].astype(jnp.float32)

    span = 32

    @pl.loop(0, n_chan * block // span)
    def _(s):
        r = s // (block // span)
        sub = lax.rem(s, block // span)
        other = (lax.rem(r, 2) - core) * (lax.rem(r, 2) - core)
        row = (other * pairs + r // 2) * block + sub * span
        rows = pl.ds(pl.multiple_of(row, span), span)
        for lane in range(wide // LANES):
            lanes = slice(lane * LANES, (lane + 1) * LANES)
            past = series[pl.ds(pl.multiple_of(s * span, span), pad + span), lanes]
            lagged = [past] + [pltpu.roll(past, TAP_SPACING * m, 0) for m in range(1, 4)]
            for b in range(bases):
                total = None
                for j in range(taps):
                    start = pad - TILE * (j // 4)
                    term = coef[b, j : j + 1, lanes] * lagged[j % 4][start : start + span]
                    total = term if total is None else total + term
                cols = slice(b * wide + lane * LANES, b * wide + (lane + 1) * LANES)
                design[rows, cols] = total.astype(design.dtype)

    def pair_copy(i):
        cols = pl.ds(pl.multiple_of(i * SLAB, SLAB), SLAB)
        return pltpu.make_async_remote_copy(
            src_ref=dsend.at[:, cols], dst_ref=drecv.at[:, cols],
            send_sem=d_send.at[i], recv_sem=d_recv.at[i],
            device_id={"chan": partner}, device_id_type=MESH,
        )

    def ring_copy(step, way, i):
        cols = pl.ds(pl.multiple_of(i * SLAB + way * half, half), half)
        return pltpu.make_async_remote_copy(
            src_ref=rsend.at[step, :, cols], dst_ref=rrecv.at[step, :, cols],
            send_sem=r_send.at[step, way, i], recv_sem=r_recv.at[step, way, i],
            device_id={"chan": (right, left)[way]}, device_id_type=MESH,
        )

    def own_part(step, way, i):
        away = pairs - 1 - step if way == 0 else step + 1
        target = lax.rem(chip + away, pairs)
        rows = pl.ds(pl.multiple_of(target * block, block), block)
        cols = pl.ds(pl.multiple_of(i * SLAB + way * half, half), half)
        return own[rows, cols]

    def ring_cols(way, i):
        return pl.ds(pl.multiple_of(i * SLAB + way * half, half), half)

    mine = pairs * block

    def multiply(i):
        weight_copy(i).wait()
        for h in range(SLAB // 256):
            cols = pl.ds(pl.multiple_of(i * SLAB + h * 256, 256), 256)
            panel = wv[:, :, cols].reshape(bases * wide, 256)
            product = jnp.dot(design[...], panel, preferred_element_type=jnp.float32)
            dsend[:, cols] = product[mine:].astype(dsend.dtype)
            own[:, cols] = product[:mine]
        pair_copy(i).start()

    def pair_sum(i):
        pair_copy(i).wait_recv()
        cols = pl.ds(pl.multiple_of(i * SLAB, SLAB), SLAB)
        own[:, cols] = own[:, cols] + drecv[:, cols].astype(jnp.float32)
        for way in range(2):
            rsend[0, :, ring_cols(way, i)] = own_part(0, way, i).astype(rsend.dtype)
            ring_copy(0, way, i).start()

    def pass_on(step, i):
        for way in range(2):
            ring_copy(step - 1, way, i).wait_recv()
            cols = ring_cols(way, i)
            total = own_part(step, way, i) + rrecv[step - 1, :, cols].astype(jnp.float32)
            if step < pairs - 1:
                rsend[step, :, cols] = total.astype(rsend.dtype)
                ring_copy(step, way, i).start()
            else:
                out_ref[:, cols] = total.astype(out_ref.dtype)

    last = 1 + (pairs - 1) * LAG

    @pl.loop(0, steps + last)
    def _(it):
        @pl.when(it < steps)
        def _():
            multiply(it)

        @pl.when(jnp.logical_and(it >= 1, it < steps + 1))
        def _():
            pair_sum(it - 1)

        for step in range(1, pairs):
            lag = 1 + step * LAG

            @pl.when(jnp.logical_and(it >= lag, it < steps + lag))
            def _(step=step, lag=lag):
                pass_on(step, it - lag)

    for d in range(1, n_chan):
        feature_copy(d).wait_send()

    @pl.loop(0, steps)
    def _(i):
        pair_copy(i).wait_send()
        for step in range(pairs - 1):
            for way in range(2):
                ring_copy(step, way, i).wait_send()


def predicted_block(features, hrf_filters, weights, n_chan):
    block, _ = features.shape
    bases, width, taps = hrf_filters.shape
    voxels = weights.shape[2]
    wide = up(width, LANES)
    steps = voxels // SLAB
    pairs = n_chan // 2
    sizes = (n_chan, bases, taps, width, wide, block, steps)
    hbm = pl.BlockSpec(memory_space=pl.ANY)
    vmem = pl.BlockSpec(memory_space=pltpu.VMEM)
    dma = pltpu.SemaphoreType.DMA
    return pl.pallas_call(
        functools.partial(main_kernel, sizes),
        out_shape=jax.ShapeDtypeStruct((block, voxels), jnp.bfloat16),
        in_specs=[hbm, vmem, hbm],
        out_specs=vmem,
        scratch_shapes=[
            pltpu.VMEM((bases, wide, voxels), jnp.bfloat16),
            pltpu.VMEM((n_chan, block, wide), jnp.bfloat16),
            pltpu.VMEM((32 + n_chan * block, wide), jnp.float32),
            pltpu.VMEM((bases, taps, wide), jnp.float32),
            pltpu.VMEM((n_chan * block, bases * wide), jnp.bfloat16),
            pltpu.VMEM((pairs * block, voxels), jnp.float32),
            pltpu.VMEM((pairs * block, voxels), jnp.bfloat16),
            pltpu.VMEM((pairs * block, voxels), jnp.bfloat16),
            pltpu.VMEM((pairs - 1, block, voxels), jnp.bfloat16),
            pltpu.VMEM((pairs - 1, block, voxels), jnp.bfloat16),
            dma((steps,)),
            dma,
            dma((n_chan - 1,)),
            dma((n_chan - 1,)),
            dma((steps,)),
            dma((steps,)),
            dma((pairs - 1, 2, steps)),
            dma((pairs - 1, 2, steps)),
        ],
        compiler_params=pltpu.CompilerParams(
            collective_id=0, has_side_effects=True, vmem_limit_bytes=VMEM_LIMIT
        ),
        name="predict",
    )(features, hrf_filters.transpose(0, 2, 1), weights)


def route_kernel(owners, cap, vp_ref, table_ref, place_ref, dest_ref):
    groups = vp_ref.shape[0]
    parcel = vp_ref[...]
    high = parcel // LANES
    low = parcel - high * LANES
    owner_parts = []
    for h in range(SORT // LANES):
        lanes = slice(h * LANES, (h + 1) * LANES)
        found = jnp.full((groups, LANES), -1, jnp.int32)
        index = low[:, lanes]
        for row in range(table_ref.shape[0]):
            entries = jnp.broadcast_to(table_ref[row : row + 1, :], (groups, LANES))
            value = jnp.take_along_axis(entries, index, axis=1)
            found = jnp.where(high[:, lanes] == row, value, found)
        owner_parts.append(found)
    owner = jnp.concatenate(owner_parts, axis=1)

    def before(n):
        return (
            lax.broadcasted_iota(jnp.int32, (n, n), 0) < lax.broadcasted_iota(jnp.int32, (n, n), 1)
        )

    def ones(mask):
        return jnp.where(mask, 1.0, 0.0).astype(jnp.bfloat16)

    ahead = ones(before(SORT))
    lane = lax.broadcasted_iota(jnp.int32, (groups, LANES), 1)
    counts = jnp.zeros((groups, LANES), jnp.float32)
    ranks = []
    for o in range(owners):
        mask = jnp.where(owner == o, 1.0, 0.0)
        ranks.append(
            jnp.dot(mask.astype(jnp.bfloat16), ahead, preferred_element_type=jnp.float32)
        )
        counts = jnp.where(lane == o, jnp.sum(mask, axis=1, keepdims=True), counts)
    earlier = ones(
        lax.broadcasted_iota(jnp.int32, (groups, groups), 0)
        > lax.broadcasted_iota(jnp.int32, (groups, groups), 1)
    )
    start = jnp.dot(earlier, counts.astype(jnp.bfloat16), preferred_element_type=jnp.float32)
    start = start.astype(jnp.int32)
    counts = counts.astype(jnp.int32)
    first = start >> 3
    phase = start & 7
    tiles = jnp.where(counts > 0, (phase + counts + 7) >> 3, 0)
    tile_start = jnp.dot(
        tiles.astype(jnp.float32).astype(jnp.bfloat16), ones(before(LANES)),
        preferred_element_type=jnp.float32,
    ).astype(jnp.int32)

    def column(values, o):
        return jnp.sum(jnp.where(lane == o, values, 0), axis=1, keepdims=True)

    place = jnp.full((groups, SORT), -1, jnp.int32)
    dest = jnp.full((groups, LANES), owners * cap // TILE, jnp.int32)
    for o in range(owners):
        offset = column(tile_start * TILE + phase, o)
        place = jnp.where(owner == o, offset + ranks[o].astype(jnp.int32), place)
        low_tile = column(tile_start, o)
        top_tile = low_tile + column(tiles, o)
        spot = o * (cap // TILE) + column(first, o) + lane - low_tile
        dest = jnp.where(jnp.logical_and(lane >= low_tile, lane < top_tile), spot, dest)
    place_ref[...] = place
    dest_ref[...] = dest


def routes(voxel_parcel, parcel_owner, owners, cap):
    voxels = voxel_parcel.shape[0]
    groups = voxels // SORT
    rows = up(groups, 8)
    parcels = jnp.pad(
        voxel_parcel.reshape(groups, SORT), ((0, rows - groups), (0, 0)), constant_values=-1
    )
    entries = up(parcel_owner.shape[0], LANES)
    table = jnp.pad(parcel_owner, (0, entries - parcel_owner.shape[0])).reshape(-1, LANES)
    return pl.pallas_call(
        functools.partial(route_kernel, owners, cap),
        out_shape=(
            jax.ShapeDtypeStruct((rows, SORT), jnp.int32),
            jax.ShapeDtypeStruct((rows, LANES), jnp.int32),
        ),
        name="route",
    )(parcels, table)


def pack_kernel(groups, owners, dest_ref, place_ref, pred_ref, out_ref, buf, loc):
    block = pred_ref.shape[0]
    zero = jnp.zeros((64, LANES), jnp.float32)

    @pl.loop(0, buf.shape[0] // 64)
    def _(i):
        buf[pl.ds(pl.multiple_of(i * 64, 64), 64), :] = zero

    local_rows = LOCAL_TILES * TILE

    @pl.loop(0, groups)
    def _(g):
        place = place_ref[pl.ds(g, 1), :]
        row = lax.broadcasted_iota(jnp.int32, (local_rows, SORT), 0)
        select = jnp.where(row == place, 1.0, 0.0).astype(jnp.bfloat16)
        part = pred_ref[:, pl.ds(pl.multiple_of(g * SORT, SORT), SORT)]
        twice = jnp.concatenate([part, part], axis=0)
        loc[...] = lax.dot_general(
            select, twice, (((1,), (1,)), ((), ())), preferred_element_type=jnp.float32
        )
        for base in range(0, LOCAL_TILES, GROUP):
            places = [
                pl.ds(pl.multiple_of(dest_ref[g, base + k] * TILE, TILE), TILE)
                for k in range(GROUP)
            ]
            held = [
                buf[spot, :] + loc[(base + k) * TILE : (base + k + 1) * TILE, :]
                for k, spot in enumerate(places)
            ]
            for spot, value in zip(places, held):
                buf[spot, :] = value

    left = lax.broadcasted_iota(jnp.int32, (LANES, LANES), 1) < block
    pairs = owners // 2
    cap = out_ref.shape[2]

    @pl.loop(0, pairs)
    def _(p):
        for tile in range(cap // LANES):
            here = pl.multiple_of(p * cap + tile * LANES, LANES)
            first = buf[pl.ds(here, LANES), :]
            second = buf[pl.ds(pl.multiple_of(pairs * cap + here, LANES), LANES), :]
            both = jnp.where(left, first, second).T.astype(out_ref.dtype)
            cols = slice(tile * LANES, (tile + 1) * LANES)
            out_ref[p, :, cols] = both[:block]
            out_ref[pairs + p, :, cols] = both[block:]


def packed_slots(predicted, place, dest, owners, cap):
    block, voxels = predicted.shape
    vmem = pl.BlockSpec(memory_space=pltpu.VMEM)
    return pl.pallas_call(
        functools.partial(pack_kernel, voxels // SORT, owners),
        out_shape=jax.ShapeDtypeStruct((owners, block, cap), jnp.bfloat16),
        in_specs=[pl.BlockSpec(memory_space=pltpu.SMEM), vmem, vmem],
        out_specs=vmem,
        scratch_shapes=[
            pltpu.VMEM((owners * cap + 64, LANES), jnp.float32),
            pltpu.VMEM((LOCAL_TILES * TILE, LANES), jnp.float32),
        ],
        compiler_params=pltpu.CompilerParams(vmem_limit_bytes=32_000_000),
        name="pack",
    )(dest, place, predicted)


def shards(features, hrf_filters, weights, voxel_parcel, parcel_owner):
    owners = lax.axis_size("vox")
    cap = 2 * voxel_parcel.shape[0] // owners
    place, dest = routes(voxel_parcel, parcel_owner, owners, cap)
    predicted = predicted_block(features, hrf_filters, weights, lax.axis_size("chan"))
    packed = packed_slots(predicted, place, dest, owners, cap)
    received = lax.all_to_all(packed, "vox", split_axis=0, concat_axis=0, tiled=True)
    return received.transpose(0, 2, 1)


def solution(mesh):
    return jax.shard_map(
        shards,
        mesh=mesh,
        in_specs=(P("chan", None), P(None, "chan", None), P(None, "chan", "vox"), P("vox"), P()),
        out_specs=P("vox", None, "chan"),
        check_vma=False,
    )
```

time: 453 us -> 96 us (0.21)
  blocking collectives: 251 us -> 26.9 us
  local copies, waits for them, and re-layouts: 149 us -> 4.78 us
  Pallas kernels: 0 us -> 63.9 us
  matrix products: 34.5 us -> 0 us
  other arithmetic: 12.4 us -> 0 us
    all_to_all x2 -> x1, blocking collectives: 251 us -> 26.9 us  [shards(): lax.all_to_all(packed, 'vox', split_axis=0, concat_axis=0, tiled=True)]
    pallas_call x0 -> x3, Pallas kernels: none -> 63.9 us  [the longest x1 53.1 us: predicted_block(): pl.pallas_call(functools.partial(main_kernel, sizes), out_shape=jax.Shape...]
    slice x18 -> x0, local copies, waits for them, and re-layouts: 52.3 us -> none  [the longest x16 51.8 us: shards(): lagged = padded[:, window_start:window_start + time_len]]
    dot_general x1 -> x0, matrix products: 34.5 us -> none  [shards(): lax.dot_general(weight_panel, design, (((0,), (0,)), ((), ())), preferred...]
    scatter x1 -> x0, local copies, waits for them, and re-layouts: 29 us -> none  [shards(): jnp.zeros((owner_count * send_cap, time_len), jnp.bfloat16).at[target_row]]
    gather x1 -> x0, local copies, waits for them, and re-layouts: 28.7 us -> none  [shards(): owners_here = jnp.take(parcel_owner, voxel_parcel)]
    reshape x1 -> x2, local copies, waits for them, and re-layouts: 17.6 us -> 2.02 us  [the longest x1 1.29 us: routes(): jnp.pad(parcel_owner, (0, entries - parcel_owner.shape[0]))]
    all_to_all x3 -> x0, local copies, waits for them, and re-layouts: 13.1 us -> none  [the longest x1 10.2 us: shards(): lax.all_to_all(packed, 'chan', split_axis=2, concat_axis=2, tiled=True)]
  transfers between devices with their start and end apart: 1 -> 0, of which waited for: 0 -> 0; matrix products, arithmetic and copies ran while one was open for 8% -> 0% of each run, Pallas kernels for 0% -> 0%
where the time goes in v1:
time: 96 us; the launch traced here: 95.7 us
  Pallas kernels  63.9 us (67%)
  blocking collectives  26.9 us (28%)
  local copies, waits for them, and re-layouts  4.78 us (5%)
    pallas_call x1, Pallas kernels, predicted_block(): pl.pallas_call(functools.partial(main_kernel, sizes), out_shape=jax.Shape...  53.1 us
    all_to_all x1, blocking collectives, shards(): lax.all_to_all(packed, 'vox', split_axis=0, concat_axis=0, tiled=True)  26.9 us
    pallas_call x1, Pallas kernels, packed_slots(): pl.pallas_call(functools.partial(pack_kernel, voxels // SORT, owners), ou...  8.29 us
    pallas_call x1, Pallas kernels, routes(): pl.pallas_call(functools.partial(route_kernel, owners, cap), out_shape=(j...  2.5 us
    unnamed x7, local copies, waits for them, and re-layouts  2.14 us

profile of v1, /device:TPU:0, one launch (start us, length us, event | category | flops | bytes accessed | tf_op | source)
XLA Modules:
  0.0 95.7 jit_solution(10149769893621273230)
XLA Ops:
  0.0 1.3 %pad_bitcast_fusion.table_ref = s32[13,128]{1,0:T(8,128)} fusion(s32[1600]{0:T(1024)} %param.9), kind=kLoop, calls=%fused_computation | loop fusion | bytes 13056 | tf_op jit(solution)/shard_map/reshape | solution.py:331
  1.3 0.7 reshape.6
  2.0 0.6 pad.8.vp_ref
  2.6 2.5 %route.1 = (s32[24,256]{1,0:T(8,128)}, s32[24,128]{1,0:T(8,128)}) custom-call(s32[24,256]{1,0:T(8,128)} %pad.8.vp_ref, s32[13,128]{1,0:T(8,128)} %pad_bitcast_fusion.table_ref), custom_call_target="tpu_custom_call" | custom-call | tf_op jit(solution)/shard_map/route/pallas_call | solution.py:332
  5.1 0.0 copy-start.1
  5.1 0.0 copy-start.2
  5.1 53.1 %predict.1.pred_ref = bf16[64,5120]{1,0:T(8,128)(2,1)} custom-call(bf16[64,5632]{1,0:T(8,128)(2,1)} %feat_ref.1, f32[3,16,704]{2,1,0:T(8,128)} %bitcast.5, bf16[3,704,5120]{2,1,0:T(8,128)(2,1)} %w_ref.1), custom_call_target="tpu_custom_call" | custom-call | tf_op jit(solution)/shard_map/predict/pallas_call | solution.py:225
  58.3 0.0 copy-done.1
  58.3 0.0 copy-done.2
  58.3 0.0 copy-start
  58.3 1.1 %copy-done = bf16[64,5120]{1,0:T(8,128)(2,1)S(1)} copy-done((bf16[64,5120]{1,0:T(8,128)(2,1)S(1)}, bf16[64,5120]{1,0:T(8,128)(2,1)}, u32[]{:S(2)}) %copy-start) | copy-done | bytes 655384
  59.4 8.3 %pack.1 = bf16[16,64,640]{2,1,0:T(8,128)(2,1)S(1)} custom-call(s32[24,128]{1,0:T(8,128)S(1)} %copy-done.2, s32[24,256]{1,0:T(8,128)S(1)} %copy-done.1, bf16[64,5120]{1,0:T(8,128)(2,1)S(1)} %copy-done), custom_call_target="tpu_custom_call" | custom-call | tf_op jit(solution)/shard_map/pack/pallas_call | solution.py:393
  67.7 26.9 %all_to_all.5 = bf16[16,64,640]{2,1,0:T(8,128)(2,1)S(1)} all-to-all(bf16[16,64,640]{2,1,0:T(8,128)(2,1)S(1)} %pack.1), channel_id=1, replica_groups=mesh['chan'=8,'vox'=16] {'vox'}, dimensions={0} | all-to-all | bytes 2621440 | tf_op jit(solution)/shard_map/all_to_all | solution.py:413
  94.6 1.1 %copy.7 = bf16[16,640,64]{1,2,0:T(8,128)(2,1)} copy(bf16[16,640,64]{1,2,0:T(8,128)(2,1)S(1)} %bitcast.4) | data formatting | bytes 2621440
Async XLA Ops:
  5.1 53.1 %copy-start.1 = (s32[24,256]{1,0:T(8,128)S(1)}, s32[24,256]{1,0:T(8,128)}, u32[]{:S(2)}) copy-start(s32[24,256]{1,0:T(8,128)} %get-tuple-element.8.place_ref) | copy-start | bytes 73732
  5.1 53.1 %copy-start.2 = (s32[24,128]{1,0:T(8,128)S(1)}, s32[24,128]{1,0:T(8,128)}, u32[]{:S(2)}) copy-start(s32[24,128]{1,0:T(8,128)} %get-tuple-element.7.dest_ref) | copy-start | bytes 36868
  58.3 1.1 %copy-start = (bf16[64,5120]{1,0:T(8,128)(2,1)S(1)}, bf16[64,5120]{1,0:T(8,128)(2,1)}, u32[]{:S(2)}) copy-start(bf16[64,5120]{1,0:T(8,128)(2,1)} %predict.1.pred_ref) | copy-start | bytes 1966084

commit v2 on v1

--- a/solution.py
+++ b/solution.py
@@ -16,7 +16,7 @@
 TILE = 8
 LOCAL_TILES = 60
 GROUP = 12
-LAG = 2
+LAGS = (1, 3, 6, 10)
 
 
 def up(value, multiple):
@@ -26,18 +26,19 @@
 def main_kernel(
     sizes,
     feat_ref, hrf_ref, w_ref, out_ref,
-    wv, fe, series, coef, design, own, dsend, drecv, rsend, rrecv,
-    w_sem, f_local, f_send, f_recv, d_send, d_recv, r_send, r_recv,
+    wv, fe, series, hrf, coef, design, own, dsend, drecv, rsend, rrecv, done,
+    w_sem, h_sem, f_local, f_send, f_recv, d_send, d_recv, r_send, r_recv, o_sem,
 ):
     n_chan, bases, taps, width, wide, block, steps = sizes
     pairs = n_chan // 2
     half = SLAB // 2
     me = lax.axis_index("chan")
     chip = me // 2
-    core = me % 2
-    partner = chip * 2 + (1 - core)
-    right = lax.rem(chip + 1, pairs) * 2 + core
-    left = lax.rem(chip + pairs - 1, pairs) * 2 + core
+    core = lax.rem(me, 2)
+
+    def device(away, flip):
+        return lax.rem(chip + away, pairs) * 2 + (core if flip == 0 else 1 - core)
+
     shift = core * (wide - width)
 
     def weight_copy(i):
@@ -51,6 +52,8 @@
 
     local = pltpu.make_async_copy(feat_ref.at[:, window(me)], fe.at[me], f_local)
     local.start()
+    taps_copy = pltpu.make_async_copy(hrf_ref, hrf, h_sem)
+    taps_copy.start()
 
     barrier = pltpu.get_barrier_semaphore()
     for d in range(1, n_chan):
@@ -59,20 +62,24 @@
         )
     pl.semaphore_wait(barrier, n_chan - 1)
 
-    def feature_copy(d):
-        peer = lax.rem(me + d, n_chan)
+    parts = [(0, 1, 0, block)]
+    parts += [(away, flip, 0, block) for away in (1, 3) for flip in (0, 1)]
+    parts += [(2, flip, row, 32) for row in (32, 0) for flip in (0, 1)]
+
+    def feature_copy(n):
+        away, flip, row, rows = parts[n]
+        peer = device(away, flip)
         return pltpu.make_async_remote_copy(
-            src_ref=feat_ref.at[:, window(peer)],
-            dst_ref=fe.at[me],
-            send_sem=f_send.at[d - 1],
-            recv_sem=f_recv.at[d - 1],
+            src_ref=feat_ref.at[pl.ds(row, rows), window(peer)],
+            dst_ref=fe.at[me, pl.ds(row, rows)],
+            send_sem=f_send.at[n],
+            recv_sem=f_recv.at[n],
             device_id={"chan": peer},
             device_id_type=MESH,
         )
 
-    for d in (4, 3, 5, 2, 6, 1, 7):
-        if d < n_chan:
-            feature_copy(d).start()
+    for n in range(len(parts)):
+        feature_copy(n).start()
 
     @pl.loop(0, steps)
     def _(i):
@@ -81,39 +88,58 @@
     blank = pl.ds(pl.multiple_of((1 - core) * width, 64), wide - width)
     for b in range(bases):
         wv[b, blank, :] = jnp.zeros((wide - width, wv.shape[2]), wv.dtype)
+    pad = 32
+    series[:pad, :] = jnp.zeros((pad, wide), jnp.float32)
+
+    def widen(source, row, rows):
+        there = pl.ds(pl.multiple_of(pad + source * block + row, 32), rows)
+        series[there, :] = fe[source, row : row + rows, :].astype(jnp.float32)
+
+    def arrive(n):
+        away, flip, row, rows = parts[n]
+        feature_copy(n).wait_recv()
+        widen(device(pairs - away, flip), row, rows)
+
+    taps_copy.wait()
     coef[...] = jnp.zeros(coef.shape, coef.dtype)
 
     @pl.when(core == 0)
     def _():
-        coef[:, :, :width] = hrf_ref[...]
+        coef[:, :, :width] = hrf[...]
 
     @pl.when(core == 1)
     def _():
-        coef[:, :, wide - width :] = hrf_ref[...]
-
-    pad = 32
-    series[:pad, :] = jnp.zeros((pad, wide), jnp.float32)
+        coef[:, :, wide - width :] = hrf[...]
+
     local.wait()
-    for d in range(1, n_chan):
-        feature_copy(d).wait_recv()
-
-    @pl.loop(0, n_chan)
-    def _(r):
-        rows = pl.ds(pl.multiple_of(pad + r * block, 32), block)
-        series[rows, :] = fe[r].astype(jnp.float32)
+    widen(me, 0, block)
+    arrive(0)
 
     span = 32
-
-    @pl.loop(0, n_chan * block // span)
+    spans = block // span
+
+    @pl.loop(0, n_chan * spans)
     def _(s):
-        r = s // (block // span)
-        sub = lax.rem(s, block // span)
-        other = (lax.rem(r, 2) - core) * (lax.rem(r, 2) - core)
+        for when, some in ((spans, (1, 2, 3, 4)), (5 * spans, (5, 6)), (6 * spans, (7, 8))):
+
+            @pl.when(s == when)
+            def _(some=some):
+                for n in some:
+                    arrive(n)
+
+        q = s // spans
+        g = q // 3
+        away = (1 + q) * (1 - g) * (2 - g) // 2 + (3 - q) * g * (2 - g) + (q - 2) * g * (g - 1) // 2
+        r = lax.rem(chip * 2 + away + n_chan, n_chan)
+        sub = lax.rem(s, spans)
+        parity = lax.rem(r, 2)
+        other = parity + core - 2 * parity * core
         row = (other * pairs + r // 2) * block + sub * span
         rows = pl.ds(pl.multiple_of(row, span), span)
+        time = pl.multiple_of(r * block + sub * span, span)
         for lane in range(wide // LANES):
             lanes = slice(lane * LANES, (lane + 1) * LANES)
-            past = series[pl.ds(pl.multiple_of(s * span, span), pad + span), lanes]
+            past = series[pl.ds(time, pad + span), lanes]
             lagged = [past] + [pltpu.roll(past, TAP_SPACING * m, 0) for m in range(1, 4)]
             for b in range(bases):
                 total = None
@@ -124,33 +150,36 @@
                 cols = slice(b * wide + lane * LANES, b * wide + (lane + 1) * LANES)
                 design[rows, cols] = total.astype(design.dtype)
 
+    mine = pairs * block
+
+    def slab(i):
+        return pl.ds(pl.multiple_of(i * SLAB, SLAB), SLAB)
+
+    def way_cols(way, i):
+        return pl.ds(pl.multiple_of(i * SLAB + way * half, half), half)
+
     def pair_copy(i):
-        cols = pl.ds(pl.multiple_of(i * SLAB, SLAB), SLAB)
         return pltpu.make_async_remote_copy(
-            src_ref=dsend.at[:, cols], dst_ref=drecv.at[:, cols],
+            src_ref=dsend.at[:, slab(i)], dst_ref=drecv.at[:, slab(i)],
             send_sem=d_send.at[i], recv_sem=d_recv.at[i],
-            device_id={"chan": partner}, device_id_type=MESH,
+            device_id={"chan": device(0, 1)}, device_id_type=MESH,
         )
 
     def ring_copy(step, way, i):
-        cols = pl.ds(pl.multiple_of(i * SLAB + way * half, half), half)
+        cols = way_cols(way, i)
         return pltpu.make_async_remote_copy(
             src_ref=rsend.at[step, :, cols], dst_ref=rrecv.at[step, :, cols],
             send_sem=r_send.at[step, way, i], recv_sem=r_recv.at[step, way, i],
-            device_id={"chan": (right, left)[way]}, device_id_type=MESH,
-        )
+            device_id={"chan": device((1, pairs - 1)[way], 0)}, device_id_type=MESH,
+        )
+
+    def out_copy(i):
+        return pltpu.make_async_copy(done.at[:, slab(i)], out_ref.at[:, slab(i)], o_sem.at[i])
 
     def own_part(step, way, i):
         away = pairs - 1 - step if way == 0 else step + 1
         target = lax.rem(chip + away, pairs)
-        rows = pl.ds(pl.multiple_of(target * block, block), block)
-        cols = pl.ds(pl.multiple_of(i * SLAB + way * half, half), half)
-        return own[rows, cols]
-
-    def ring_cols(way, i):
-        return pl.ds(pl.multiple_of(i * SLAB + way * half, half), half)
-
-    mine = pairs * block
+        return own[pl.ds(pl.multiple_of(target * block, block), block), way_cols(way, i)]
 
     def multiply(i):
         weight_copy(i).wait()
@@ -164,44 +193,40 @@
 
     def pair_sum(i):
         pair_copy(i).wait_recv()
-        cols = pl.ds(pl.multiple_of(i * SLAB, SLAB), SLAB)
-        own[:, cols] = own[:, cols] + drecv[:, cols].astype(jnp.float32)
-        for way in range(2):
-            rsend[0, :, ring_cols(way, i)] = own_part(0, way, i).astype(rsend.dtype)
-            ring_copy(0, way, i).start()
+        own[:, slab(i)] = own[:, slab(i)] + drecv[:, slab(i)].astype(jnp.float32)
 
     def pass_on(step, i):
         for way in range(2):
-            ring_copy(step - 1, way, i).wait_recv()
-            cols = ring_cols(way, i)
-            total = own_part(step, way, i) + rrecv[step - 1, :, cols].astype(jnp.float32)
+            cols = way_cols(way, i)
+            total = own_part(step, way, i)
+            if step > 0:
+                ring_copy(step - 1, way, i).wait_recv()
+                total = total + rrecv[step - 1, :, cols].astype(jnp.float32)
             if step < pairs - 1:
                 rsend[step, :, cols] = total.astype(rsend.dtype)
                 ring_copy(step, way, i).start()
             else:
-                out_ref[:, cols] = total.astype(out_ref.dtype)
-
-    last = 1 + (pairs - 1) * LAG
-
-    @pl.loop(0, steps + last)
+                done[:, cols] = total.astype(done.dtype)
+        if step == pairs - 1:
+            out_copy(i).start()
+
+    @pl.loop(0, steps + LAGS[-1])
     def _(it):
         @pl.when(it < steps)
         def _():
             multiply(it)
 
-        @pl.when(jnp.logical_and(it >= 1, it < steps + 1))
-        def _():
-            pair_sum(it - 1)
-
-        for step in range(1, pairs):
-            lag = 1 + step * LAG
+        for step in range(pairs):
+            lag = LAGS[step]
 
             @pl.when(jnp.logical_and(it >= lag, it < steps + lag))
             def _(step=step, lag=lag):
+                if step == 0:
+                    pair_sum(it - lag)
                 pass_on(step, it - lag)
 
-    for d in range(1, n_chan):
-        feature_copy(d).wait_send()
+    for n in range(len(parts)):
+        feature_copy(n).wait_send()
 
     @pl.loop(0, steps)
     def _(i):
@@ -209,6 +234,7 @@
         for step in range(pairs - 1):
             for way in range(2):
                 ring_copy(step, way, i).wait_send()
+        out_copy(i).wait()
 
 
 def predicted_block(features, hrf_filters, weights, n_chan):
@@ -220,17 +246,17 @@
     pairs = n_chan // 2
     sizes = (n_chan, bases, taps, width, wide, block, steps)
     hbm = pl.BlockSpec(memory_space=pl.ANY)
-    vmem = pl.BlockSpec(memory_space=pltpu.VMEM)
     dma = pltpu.SemaphoreType.DMA
     return pl.pallas_call(
         functools.partial(main_kernel, sizes),
         out_shape=jax.ShapeDtypeStruct((block, voxels), jnp.bfloat16),
-        in_specs=[hbm, vmem, hbm],
-        out_specs=vmem,
+        in_specs=[hbm, hbm, hbm],
+        out_specs=hbm,
         scratch_shapes=[
             pltpu.VMEM((bases, wide, voxels), jnp.bfloat16),
             pltpu.VMEM((n_chan, block, wide), jnp.bfloat16),
             pltpu.VMEM((32 + n_chan * block, wide), jnp.float32),
+            pltpu.VMEM((bases, taps, width), jnp.float32),
             pltpu.VMEM((bases, taps, wide), jnp.float32),
             pltpu.VMEM((n_chan * block, bases * wide), jnp.bfloat16),
             pltpu.VMEM((pairs * block, voxels), jnp.float32),
@@ -238,14 +264,17 @@
             pltpu.VMEM((pairs * block, voxels), jnp.bfloat16),
             pltpu.VMEM((pairs - 1, block, voxels), jnp.bfloat16),
             pltpu.VMEM((pairs - 1, block, voxels), jnp.bfloat16),
+            pltpu.VMEM((block, voxels), jnp.bfloat16),
             dma((steps,)),
             dma,
-            dma((n_chan - 1,)),
-            dma((n_chan - 1,)),
+            dma,
+            dma((n_chan + 1,)),
+            dma((n_chan + 1,)),
             dma((steps,)),
             dma((steps,)),
             dma((pairs - 1, 2, steps)),
             dma((pairs - 1, 2, steps)),
+            dma((steps,)),
         ],
         compiler_params=pltpu.CompilerParams(
             collective_id=0, has_side_effects=True, vmem_limit_bytes=VMEM_LIMIT
@@ -339,8 +368,10 @@
     )(parcels, table)
 
 
-def pack_kernel(groups, owners, dest_ref, place_ref, pred_ref, out_ref, buf, loc):
+def pack_kernel(groups, owners, dest_ref, place_ref, pred_hbm, out_ref, pred_ref, buf, loc, sem):
     block = pred_ref.shape[0]
+    fetch = pltpu.make_async_copy(pred_hbm, pred_ref, sem)
+    fetch.start()
     zero = jnp.zeros((64, LANES), jnp.float32)
 
     @pl.loop(0, buf.shape[0] // 64)
@@ -348,6 +379,7 @@
         buf[pl.ds(pl.multiple_of(i * 64, 64), 64), :] = zero
 
     local_rows = LOCAL_TILES * TILE
+    fetch.wait()
 
     @pl.loop(0, groups)
     def _(g):
@@ -371,20 +403,25 @@
             for spot, value in zip(places, held):
                 buf[spot, :] = value
 
-    left = lax.broadcasted_iota(jnp.int32, (LANES, LANES), 1) < block
     pairs = owners // 2
     cap = out_ref.shape[2]
+    left = lax.broadcasted_iota(jnp.int32, (cap, LANES), 1) < block
+    unit = jnp.where(
+        lax.broadcasted_iota(jnp.int32, (LANES, LANES), 0)
+        == lax.broadcasted_iota(jnp.int32, (LANES, LANES), 1),
+        1.0, 0.0,
+    ).astype(jnp.bfloat16)
 
     @pl.loop(0, pairs)
     def _(p):
-        for tile in range(cap // LANES):
-            here = pl.multiple_of(p * cap + tile * LANES, LANES)
-            first = buf[pl.ds(here, LANES), :]
-            second = buf[pl.ds(pl.multiple_of(pairs * cap + here, LANES), LANES), :]
-            both = jnp.where(left, first, second).T.astype(out_ref.dtype)
-            cols = slice(tile * LANES, (tile + 1) * LANES)
-            out_ref[p, :, cols] = both[:block]
-            out_ref[pairs + p, :, cols] = both[block:]
+        first = buf[pl.ds(pl.multiple_of(p * cap, LANES), cap), :]
+        second = buf[pl.ds(pl.multiple_of((pairs + p) * cap, LANES), cap), :]
+        both = jnp.where(left, first, second).astype(jnp.bfloat16)
+        turned = lax.dot_general(
+            unit, both, (((1,), (1,)), ((), ())), preferred_element_type=jnp.float32
+        ).astype(out_ref.dtype)
+        out_ref[p] = turned[:block]
+        out_ref[pairs + p] = turned[block:]
 
 
 def packed_slots(predicted, place, dest, owners, cap):
@@ -393,15 +430,60 @@
     return pl.pallas_call(
         functools.partial(pack_kernel, voxels // SORT, owners),
         out_shape=jax.ShapeDtypeStruct((owners, block, cap), jnp.bfloat16),
-        in_specs=[pl.BlockSpec(memory_space=pltpu.SMEM), vmem, vmem],
+        in_specs=[
+            pl.BlockSpec(memory_space=pltpu.SMEM), vmem, pl.BlockSpec(memory_space=pltpu.HBM)
+        ],
         out_specs=vmem,
         scratch_shapes=[
+            pltpu.VMEM((block, voxels), predicted.dtype),
             pltpu.VMEM((owners * cap + 64, LANES), jnp.float32),
             pltpu.VMEM((LOCAL_TILES * TILE, LANES), jnp.float32),
+            pltpu.SemaphoreType.DMA,
         ],
-        compiler_params=pltpu.CompilerParams(vmem_limit_bytes=32_000_000),
+        compiler_params=pltpu.CompilerParams(vmem_limit_bytes=16_000_000),
         name="pack",
     )(dest, place, predicted)
+
+
+def exchange_kernel(n, in_ref, out_ref, local_sem, send_sem, recv_sem):
+    me = lax.axis_index("vox")
+    local = pltpu.make_async_copy(in_ref.at[me], out_ref.at[me], local_sem)
+    local.start()
+    barrier = pltpu.get_barrier_semaphore()
+    for d in range(1, n):
+        pl.semaphore_signal(
+            barrier, inc=1, device_id={"vox": lax.rem(me + d, n)}, device_id_type=MESH
+        )
+    pl.semaphore_wait(barrier, n - 1)
+
+    def block_copy(d):
+        peer = lax.rem(me + d, n)
+        return pltpu.make_async_remote_copy(
+            src_ref=in_ref.at[peer], dst_ref=out_ref.at[me],
+            send_sem=send_sem.at[d - 1], recv_sem=recv_sem.at[d - 1],
+            device_id={"vox": peer}, device_id_type=MESH,
+        )
+
+    for d in range(1, n):
+        block_copy(d).start()
+    local.wait()
+    for d in range(1, n):
+        block_copy(d).wait()
+
+
+def exchange(packed, n):
+    dma = pltpu.SemaphoreType.DMA
+    return pl.pallas_call(
+        functools.partial(exchange_kernel, n),
+        out_shape=jax.ShapeDtypeStruct(packed.shape, packed.dtype),
+        in_specs=[pl.BlockSpec(memory_space=pl.ANY)],
+        out_specs=pl.BlockSpec(memory_space=pl.ANY),
+        scratch_shapes=[dma, dma((n - 1,)), dma((n - 1,))],
+        compiler_params=pltpu.CompilerParams(
+            collective_id=1, has_side_effects=True, vmem_limit_bytes=4_000_000
+        ),
+        name="exchange",
+    )(packed)
 
 
 def shards(features, hrf_filters, weights, voxel_parcel, parcel_owner):
@@ -410,8 +492,7 @@
     place, dest = routes(voxel_parcel, parcel_owner, owners, cap)
     predicted = predicted_block(features, hrf_filters, weights, lax.axis_size("chan"))
     packed = packed_slots(predicted, place, dest, owners, cap)
-    received = lax.all_to_all(packed, "vox", split_axis=0, concat_axis=0, tiled=True)
-    return received.transpose(0, 2, 1)
+    return exchange(packed, owners).transpose(0, 2, 1)
 
 
 def solution(mesh):

time: 96 us -> 87.3 us (0.909)
  blocking collectives: 26.9 us -> 0 us
  Pallas kernels: 63.9 us -> 82.2 us
    all_to_all x1 -> x0, blocking collectives: 26.9 us -> none  [shards(): lax.all_to_all(packed, 'vox', split_axis=0, concat_axis=0, tiled=True)]
    pallas_call x0 -> x1, Pallas kernels: none -> 23.1 us  [exchange(): pl.pallas_call(functools.partial(exchange_kernel, n), out_shape=jax.Shape...]
    pallas_call x1, Pallas kernels: 53.1 us -> 47.5 us  [predicted_block(): pl.pallas_call(functools.partial(main_kernel, sizes), out_shape=jax.Shape...]
where the time goes in v2:
time: 87.3 us; the launch traced here: 87 us
  Pallas kernels  82.2 us (94%)
  local copies, waits for them, and re-layouts  4.79 us (5%)
    pallas_call x1, Pallas kernels, predicted_block(): pl.pallas_call(functools.partial(main_kernel, sizes), out_shape=jax.Shape...  47.5 us
    pallas_call x1, Pallas kernels, exchange(): pl.pallas_call(functools.partial(exchange_kernel, n), out_shape=jax.Shape...  23.1 us
    pallas_call x1, Pallas kernels, packed_slots(): pl.pallas_call(functools.partial(pack_kernel, voxels // SORT, owners), ou...  9.05 us
    pallas_call x1, Pallas kernels, routes(): pl.pallas_call(functools.partial(route_kernel, owners, cap), out_shape=(j...  2.5 us
    unnamed x7, local copies, waits for them, and re-layouts  2.15 us

profile of v2, /device:TPU:0, one launch (start us, length us, event | category | flops | bytes accessed | tf_op | source)
XLA Modules:
  0.0 87.0 jit_solution(6170522823562651943)
XLA Ops:
  0.0 1.3 %pad_bitcast_fusion.table_ref = s32[13,128]{1,0:T(8,128)} fusion(s32[1600]{0:T(1024)} %param.9), kind=kLoop, calls=%fused_computation | loop fusion | bytes 13056 | tf_op jit(solution)/shard_map/reshape | solution.py:360
  1.3 0.7 reshape.6
  2.0 0.6 pad.8.vp_ref
  2.6 2.5 %route.1 = (s32[24,256]{1,0:T(8,128)}, s32[24,128]{1,0:T(8,128)}) custom-call(s32[24,256]{1,0:T(8,128)} %pad.8.vp_ref, s32[13,128]{1,0:T(8,128)} %pad_bitcast_fusion.table_ref), custom_call_target="tpu_custom_call" | custom-call | tf_op jit(solution)/shard_map/route/pallas_call | solution.py:361
  5.1 0.0 copy-start.1
  5.1 0.0 copy-start.2
  5.1 47.5 %predict.1.pred_hbm = bf16[64,5120]{1,0:T(8,128)(2,1)} custom-call(bf16[64,5632]{1,0:T(8,128)(2,1)} %feat_ref.1, f32[3,16,704]{2,1,0:T(8,128)} %bitcast.5, bf16[3,704,5120]{2,1,0:T(8,128)(2,1)} %w_ref.1), custom_call_target="tpu_custom_call" | custom-call | tf_op jit(solution)/shard_map/predict/pallas_call | solution.py:250
  52.6 0.0 copy-done.1
  52.6 0.0 copy-done.2
  52.6 0.0 copy-start
  52.7 1.1 %copy-done = bf16[64,5120]{1,0:T(8,128)(2,1)S(1)} copy-done((bf16[64,5120]{1,0:T(8,128)(2,1)S(1)}, bf16[64,5120]{1,0:T(8,128)(2,1)}, u32[]{:S(2)}) %copy-start) | copy-done | bytes 655384
  53.7 9.1 %pack.1.in_ref = bf16[16,64,640]{2,1,0:T(8,128)(2,1)S(1)} custom-call(s32[24,128]{1,0:T(8,128)S(1)} %copy-done.2, s32[24,256]{1,0:T(8,128)S(1)} %copy-done.1, bf16[64,5120]{1,0:T(8,128)(2,1)S(1)} %copy-done), custom_call_target="tpu_custom_call" | custom-call | tf_op jit(solution)/shard_map/pack/pallas_call | solution.py:430
  62.8 23.1 %exchange.1 = bf16[16,64,640]{2,1,0:T(8,128)(2,1)S(1)} custom-call(bf16[16,64,640]{2,1,0:T(8,128)(2,1)S(1)} %pack.1.in_ref), custom_call_target="tpu_custom_call" | custom-call | tf_op jit(solution)/shard_map/exchange/pallas_call | solution.py:476
  85.9 1.1 %copy.7 = bf16[16,640,64]{1,2,0:T(8,128)(2,1)} copy(bf16[16,640,64]{1,2,0:T(8,128)(2,1)S(1)} %bitcast.4) | data formatting | bytes 2621440
Async XLA Ops:
  5.1 47.5 %copy-start.1 = (s32[24,256]{1,0:T(8,128)S(1)}, s32[24,256]{1,0:T(8,128)}, u32[]{:S(2)}) copy-start(s32[24,256]{1,0:T(8,128)} %get-tuple-element.8.place_ref) | copy-start | bytes 73732
  5.1 47.5 %copy-start.2 = (s32[24,128]{1,0:T(8,128)S(1)}, s32[24,128]{1,0:T(8,128)}, u32[]{:S(2)}) copy-start(s32[24,128]{1,0:T(8,128)} %get-tuple-element.7.dest_ref) | copy-start | bytes 36868
  52.6 1.1 %copy-start = (bf16[64,5120]{1,0:T(8,128)(2,1)S(1)}, bf16[64,5120]{1,0:T(8,128)(2,1)}, u32[]{:S(2)}) copy-start(bf16[64,5120]{1,0:T(8,128)(2,1)} %predict.1.pred_hbm) | copy-start | bytes 1966084

commit v3 on v2

--- a/solution.py
+++ b/solution.py
@@ -23,13 +23,70 @@
     return -(-value // multiple) * multiple
 
 
+def ones(mask):
+    return jnp.where(mask, 1.0, 0.0).astype(jnp.bfloat16)
+
+
+def route(owners, cap, parcel_ref, table_ref, place_ref, dest_ref):
+    rows = parcel_ref.shape[0]
+    parcel = parcel_ref[...]
+    high = parcel >> 7
+    low = parcel & (LANES - 1)
+    owner = jnp.zeros((rows, LANES), jnp.int32)
+    for row in range(table_ref.shape[0]):
+        line = jnp.broadcast_to(table_ref[row : row + 1, :], (rows, LANES))
+        owner = jnp.where(high == row, jnp.take_along_axis(line, low, axis=1), owner)
+
+    def iotas(n):
+        shape = (n, n)
+        return (
+            lax.broadcasted_iota(jnp.int32, shape, 0), lax.broadcasted_iota(jnp.int32, shape, 1)
+        )
+
+    def dot(a, b):
+        return jnp.dot(a, b, preferred_element_type=jnp.float32)
+
+    first, second = iotas(LANES)
+    ahead = ones(first < second)
+    lane = lax.broadcasted_iota(jnp.int32, (rows, LANES), 1)
+    counts = jnp.zeros((rows, LANES), jnp.float32)
+    ranks = []
+    for o in range(owners):
+        mask = jnp.where(owner == o, 1.0, 0.0)
+        ranks.append(dot(mask.astype(jnp.bfloat16), ahead))
+        counts = jnp.where(lane == o, jnp.sum(mask, axis=1, keepdims=True), counts)
+    counts = counts.astype(jnp.bfloat16)
+    first, second = iotas(rows)
+    start = dot(ones(second < first), counts).astype(jnp.int32)
+    base = dot(ones((second >> 1) < (first >> 1)), counts).astype(jnp.int32)
+    count = dot(ones((second >> 1) == (first >> 1)), counts).astype(jnp.int32)
+    tile = base >> 3
+    tiles = jnp.where(count > 0, ((base & 7) + count + 7) >> 3, 0)
+    tile_start = dot(tiles.astype(jnp.float32).astype(jnp.bfloat16), ahead).astype(jnp.int32)
+
+    def column(values, o):
+        return jnp.sum(jnp.where(lane == o, values, 0), axis=1, keepdims=True)
+
+    place = jnp.zeros((rows, LANES), jnp.int32)
+    dest = jnp.full((rows, LANES), owners * cap // TILE, jnp.int32)
+    offsets = (tile_start - tile) * TILE + start
+    for o in range(owners):
+        place = jnp.where(owner == o, column(offsets, o) + ranks[o].astype(jnp.int32), place)
+        low_tile = column(tile_start, o)
+        top_tile = low_tile + column(tiles, o)
+        spot = o * (cap // TILE) + column(tile, o) + lane - low_tile
+        dest = jnp.where(jnp.logical_and(lane >= low_tile, lane < top_tile), spot, dest)
+    place_ref[...] = place
+    dest_ref[...] = dest
+
+
 def main_kernel(
     sizes,
-    feat_ref, hrf_ref, w_ref, out_ref,
-    wv, fe, series, hrf, coef, design, own, dsend, drecv, rsend, rrecv, done,
+    feat_ref, hrf_ref, w_ref, parcel_ref, table_ref, sorted_ref, dest_ref,
+    wv, fe, series, hrf, coef, design, own, dsend, drecv, rsend, rrecv, place, ordered,
     w_sem, h_sem, f_local, f_send, f_recv, d_send, d_recv, r_send, r_recv, o_sem,
 ):
-    n_chan, bases, taps, width, wide, block, steps = sizes
+    n_chan, bases, taps, width, wide, block, steps, owners, cap = sizes
     pairs = n_chan // 2
     half = SLAB // 2
     me = lax.axis_index("chan")
@@ -114,6 +171,7 @@
     local.wait()
     widen(me, 0, block)
     arrive(0)
+    route(owners, cap, parcel_ref, table_ref, place, dest_ref)
 
     span = 32
     spans = block // span
@@ -173,8 +231,26 @@
             device_id={"chan": device((1, pairs - 1)[way], 0)}, device_id_type=MESH,
         )
 
+    local_rows = LOCAL_TILES * TILE
+    slab_groups = SLAB // SORT
+
     def out_copy(i):
-        return pltpu.make_async_copy(done.at[:, slab(i)], out_ref.at[:, slab(i)], o_sem.at[i])
+        size = slab_groups * local_rows
+        rows = pl.ds(pl.multiple_of(i * size, 16), size)
+        return pltpu.make_async_copy(ordered.at[rows], sorted_ref.at[rows], o_sem.at[i])
+
+    def sort_group(i, k, values):
+        group = i * slab_groups + k
+        spots = lax.broadcasted_iota(jnp.int32, (local_rows, LANES), 0)
+        select = jnp.concatenate(
+            [ones(spots == place[pl.ds(2 * group + h, 1), :]) for h in range(2)], axis=1
+        )
+        twice = jnp.concatenate([values, values], axis=0)
+        rows = lax.dot_general(
+            select, twice, (((1,), (1,)), ((), ())), preferred_element_type=jnp.float32
+        )
+        here = pl.ds(pl.multiple_of(group * local_rows, 16), local_rows)
+        ordered[here, :] = rows.astype(ordered.dtype)
 
     def own_part(step, way, i):
         away = pairs - 1 - step if way == 0 else step + 1
@@ -206,7 +282,7 @@
                 rsend[step, :, cols] = total.astype(rsend.dtype)
                 ring_copy(step, way, i).start()
             else:
-                done[:, cols] = total.astype(done.dtype)
+                sort_group(i, way, total.astype(jnp.bfloat16))
         if step == pairs - 1:
             out_copy(i).start()
 
@@ -237,21 +313,30 @@
         out_copy(i).wait()
 
 
-def predicted_block(features, hrf_filters, weights, n_chan):
+def sorted_block(features, hrf_filters, weights, voxel_parcel, parcel_owner, n_chan, owners):
     block, _ = features.shape
     bases, width, taps = hrf_filters.shape
     voxels = weights.shape[2]
     wide = up(width, LANES)
     steps = voxels // SLAB
     pairs = n_chan // 2
-    sizes = (n_chan, bases, taps, width, wide, block, steps)
+    cap = 2 * voxels // owners
+    sizes = (n_chan, bases, taps, width, wide, block, steps, owners, cap)
+    parcels = voxel_parcel.reshape(-1, LANES)
+    entries = up(parcel_owner.shape[0], LANES)
+    table = jnp.pad(parcel_owner, (0, entries - parcel_owner.shape[0])).reshape(-1, LANES)
+    sorted_rows = voxels // SORT * LOCAL_TILES * TILE
     hbm = pl.BlockSpec(memory_space=pl.ANY)
+    vmem = pl.BlockSpec(memory_space=pltpu.VMEM)
     dma = pltpu.SemaphoreType.DMA
     return pl.pallas_call(
         functools.partial(main_kernel, sizes),
-        out_shape=jax.ShapeDtypeStruct((block, voxels), jnp.bfloat16),
-        in_specs=[hbm, hbm, hbm],
-        out_specs=hbm,
+        out_shape=(
+            jax.ShapeDtypeStruct((sorted_rows, 2 * block), jnp.bfloat16),
+            jax.ShapeDtypeStruct(parcels.shape, jnp.int32),
+        ),
+        in_specs=[hbm, hbm, hbm, vmem, vmem],
+        out_specs=(hbm, vmem),
         scratch_shapes=[
             pltpu.VMEM((bases, wide, voxels), jnp.bfloat16),
             pltpu.VMEM((n_chan, block, wide), jnp.bfloat16),
@@ -264,7 +349,8 @@
             pltpu.VMEM((pairs * block, voxels), jnp.bfloat16),
             pltpu.VMEM((pairs - 1, block, voxels), jnp.bfloat16),
             pltpu.VMEM((pairs - 1, block, voxels), jnp.bfloat16),
-            pltpu.VMEM((block, voxels), jnp.bfloat16),
+            pltpu.VMEM(parcels.shape, jnp.int32),
+            pltpu.VMEM((sorted_rows, 2 * block), jnp.bfloat16),
             dma((steps,)),
             dma,
             dma,
@@ -280,128 +366,44 @@
             collective_id=0, has_side_effects=True, vmem_limit_bytes=VMEM_LIMIT
         ),
         name="predict",
-    )(features, hrf_filters.transpose(0, 2, 1), weights)
-
-
-def route_kernel(owners, cap, vp_ref, table_ref, place_ref, dest_ref):
-    groups = vp_ref.shape[0]
-    parcel = vp_ref[...]
-    high = parcel // LANES
-    low = parcel - high * LANES
-    owner_parts = []
-    for h in range(SORT // LANES):
-        lanes = slice(h * LANES, (h + 1) * LANES)
-        found = jnp.full((groups, LANES), -1, jnp.int32)
-        index = low[:, lanes]
-        for row in range(table_ref.shape[0]):
-            entries = jnp.broadcast_to(table_ref[row : row + 1, :], (groups, LANES))
-            value = jnp.take_along_axis(entries, index, axis=1)
-            found = jnp.where(high[:, lanes] == row, value, found)
-        owner_parts.append(found)
-    owner = jnp.concatenate(owner_parts, axis=1)
-
-    def before(n):
-        return (
-            lax.broadcasted_iota(jnp.int32, (n, n), 0) < lax.broadcasted_iota(jnp.int32, (n, n), 1)
-        )
-
-    def ones(mask):
-        return jnp.where(mask, 1.0, 0.0).astype(jnp.bfloat16)
-
-    ahead = ones(before(SORT))
-    lane = lax.broadcasted_iota(jnp.int32, (groups, LANES), 1)
-    counts = jnp.zeros((groups, LANES), jnp.float32)
-    ranks = []
-    for o in range(owners):
-        mask = jnp.where(owner == o, 1.0, 0.0)
-        ranks.append(
-            jnp.dot(mask.astype(jnp.bfloat16), ahead, preferred_element_type=jnp.float32)
-        )
-        counts = jnp.where(lane == o, jnp.sum(mask, axis=1, keepdims=True), counts)
-    earlier = ones(
-        lax.broadcasted_iota(jnp.int32, (groups, groups), 0)
-        > lax.broadcasted_iota(jnp.int32, (groups, groups), 1)
-    )
-    start = jnp.dot(earlier, counts.astype(jnp.bfloat16), preferred_element_type=jnp.float32)
-    start = start.astype(jnp.int32)
-    counts = counts.astype(jnp.int32)
-    first = start >> 3
-    phase = start & 7
-    tiles = jnp.where(counts > 0, (phase + counts + 7) >> 3, 0)
-    tile_start = jnp.dot(
-        tiles.astype(jnp.float32).astype(jnp.bfloat16), ones(before(LANES)),
-        preferred_element_type=jnp.float32,
-    ).astype(jnp.int32)
-
-    def column(values, o):
-        return jnp.sum(jnp.where(lane == o, values, 0), axis=1, keepdims=True)
-
-    place = jnp.full((groups, SORT), -1, jnp.int32)
-    dest = jnp.full((groups, LANES), owners * cap // TILE, jnp.int32)
-    for o in range(owners):
-        offset = column(tile_start * TILE + phase, o)
-        place = jnp.where(owner == o, offset + ranks[o].astype(jnp.int32), place)
-        low_tile = column(tile_start, o)
-        top_tile = low_tile + column(tiles, o)
-        spot = o * (cap // TILE) + column(first, o) + lane - low_tile
-        dest = jnp.where(jnp.logical_and(lane >= low_tile, lane < top_tile), spot, dest)
-    place_ref[...] = place
-    dest_ref[...] = dest
-
-
-def routes(voxel_parcel, parcel_owner, owners, cap):
-    voxels = voxel_parcel.shape[0]
-    groups = voxels // SORT
-    rows = up(groups, 8)
-    parcels = jnp.pad(
-        voxel_parcel.reshape(groups, SORT), ((0, rows - groups), (0, 0)), constant_values=-1
-    )
-    entries = up(parcel_owner.shape[0], LANES)
-    table = jnp.pad(parcel_owner, (0, entries - parcel_owner.shape[0])).reshape(-1, LANES)
-    return pl.pallas_call(
-        functools.partial(route_kernel, owners, cap),
-        out_shape=(
-            jax.ShapeDtypeStruct((rows, SORT), jnp.int32),
-            jax.ShapeDtypeStruct((rows, LANES), jnp.int32),
-        ),
-        name="route",
-    )(parcels, table)
-
-
-def pack_kernel(groups, owners, dest_ref, place_ref, pred_hbm, out_ref, pred_ref, buf, loc, sem):
-    block = pred_ref.shape[0]
-    fetch = pltpu.make_async_copy(pred_hbm, pred_ref, sem)
-    fetch.start()
+    )(features, hrf_filters.transpose(0, 2, 1), weights, parcels, table)
+
+
+def pack_kernel(groups, owners, block, dest_ref, sorted_hbm, out_ref, held, buf, sem):
+    local_rows = LOCAL_TILES * TILE
+    parts = sem.shape[0]
+    size = groups * local_rows // parts
+
+    def fetch(k):
+        here = pl.ds(k * size, size)
+        return pltpu.make_async_copy(sorted_hbm.at[here], held.at[here], sem.at[k])
+
+    for k in range(parts):
+        fetch(k).start()
     zero = jnp.zeros((64, LANES), jnp.float32)
 
     @pl.loop(0, buf.shape[0] // 64)
     def _(i):
         buf[pl.ds(pl.multiple_of(i * 64, 64), 64), :] = zero
 
-    local_rows = LOCAL_TILES * TILE
-    fetch.wait()
-
-    @pl.loop(0, groups)
-    def _(g):
-        place = place_ref[pl.ds(g, 1), :]
-        row = lax.broadcasted_iota(jnp.int32, (local_rows, SORT), 0)
-        select = jnp.where(row == place, 1.0, 0.0).astype(jnp.bfloat16)
-        part = pred_ref[:, pl.ds(pl.multiple_of(g * SORT, SORT), SORT)]
-        twice = jnp.concatenate([part, part], axis=0)
-        loc[...] = lax.dot_general(
-            select, twice, (((1,), (1,)), ((), ())), preferred_element_type=jnp.float32
-        )
-        for base in range(0, LOCAL_TILES, GROUP):
-            places = [
-                pl.ds(pl.multiple_of(dest_ref[g, base + k] * TILE, TILE), TILE)
-                for k in range(GROUP)
-            ]
-            held = [
-                buf[spot, :] + loc[(base + k) * TILE : (base + k + 1) * TILE, :]
-                for k, spot in enumerate(places)
-            ]
-            for spot, value in zip(places, held):
-                buf[spot, :] = value
+    for k in range(parts):
+        fetch(k).wait()
+
+        @pl.loop(k * groups // parts, (k + 1) * groups // parts)
+        def _(g):
+            for base in range(0, LOCAL_TILES, GROUP):
+                start = pl.multiple_of(g * local_rows + base * TILE, 2 * TILE)
+                added = held[pl.ds(start, GROUP * TILE), :].astype(jnp.float32)
+                places = [
+                    pl.ds(pl.multiple_of(dest_ref[2 * g, base + n] * TILE, TILE), TILE)
+                    for n in range(GROUP)
+                ]
+                sums = [
+                    buf[spot, :] + added[n * TILE : (n + 1) * TILE]
+                    for n, spot in enumerate(places)
+                ]
+                for spot, value in zip(places, sums):
+                    buf[spot, :] = value
 
     pairs = owners // 2
     cap = out_ref.shape[2]
@@ -424,29 +426,28 @@
         out_ref[pairs + p] = turned[block:]
 
 
-def packed_slots(predicted, place, dest, owners, cap):
-    block, voxels = predicted.shape
-    vmem = pl.BlockSpec(memory_space=pltpu.VMEM)
+def packed_slots(sorted_rows, dest, block, owners, cap):
+    rows = sorted_rows.shape[0]
+    groups = rows // (LOCAL_TILES * TILE)
+    hbm = pl.BlockSpec(memory_space=pl.ANY)
     return pl.pallas_call(
-        functools.partial(pack_kernel, voxels // SORT, owners),
+        functools.partial(pack_kernel, groups, owners, block),
         out_shape=jax.ShapeDtypeStruct((owners, block, cap), jnp.bfloat16),
-        in_specs=[
-            pl.BlockSpec(memory_space=pltpu.SMEM), vmem, pl.BlockSpec(memory_space=pltpu.HBM)
+        in_specs=[pl.BlockSpec(memory_space=pltpu.SMEM), hbm],
+        out_specs=pl.BlockSpec(memory_space=pltpu.VMEM),
+        scratch_shapes=[
+            pltpu.VMEM(sorted_rows.shape, sorted_rows.dtype),
+            pltpu.VMEM((owners * cap + 64, LANES), jnp.float32),
+            pltpu.SemaphoreType.DMA((4,)),
         ],
-        out_specs=vmem,
-        scratch_shapes=[
-            pltpu.VMEM((block, voxels), predicted.dtype),
-            pltpu.VMEM((owners * cap + 64, LANES), jnp.float32),
-            pltpu.VMEM((LOCAL_TILES * TILE, LANES), jnp.float32),
-            pltpu.SemaphoreType.DMA,
-        ],
-        compiler_params=pltpu.CompilerParams(vmem_limit_bytes=16_000_000),
+        compiler_params=pltpu.CompilerParams(vmem_limit_bytes=60_000_000),
         name="pack",
-    )(dest, place, predicted)
+    )(dest, sorted_rows)
 
 
 def exchange_kernel(n, in_ref, out_ref, local_sem, send_sem, recv_sem):
     me = lax.axis_index("vox")
+    side = 4
     local = pltpu.make_async_copy(in_ref.at[me], out_ref.at[me], local_sem)
     local.start()
     barrier = pltpu.get_barrier_semaphore()
@@ -457,14 +458,16 @@
     pl.semaphore_wait(barrier, n - 1)
 
     def block_copy(d):
-        peer = lax.rem(me + d, n)
+        up_z, up_y = divmod(d, side)
+        peer = lax.rem(me // side + up_z, n // side) * side + lax.rem(me + up_y, side)
         return pltpu.make_async_remote_copy(
             src_ref=in_ref.at[peer], dst_ref=out_ref.at[me],
             send_sem=send_sem.at[d - 1], recv_sem=recv_sem.at[d - 1],
             device_id={"vox": peer}, device_id_type=MESH,
         )
 
-    for d in range(1, n):
+    apart = {d: sum(min(k, side - k) for k in divmod(d, side)) for d in range(1, n)}
+    for d in sorted(apart, key=lambda d: -apart[d]):
         block_copy(d).start()
     local.wait()
     for d in range(1, n):
@@ -480,7 +483,7 @@
         out_specs=pl.BlockSpec(memory_space=pl.ANY),
         scratch_shapes=[dma, dma((n - 1,)), dma((n - 1,))],
         compiler_params=pltpu.CompilerParams(
-            collective_id=1, has_side_effects=True, vmem_limit_bytes=4_000_000
+            collective_id=1, has_side_effects=True, vmem_limit_bytes=60_000_000
         ),
         name="exchange",
     )(packed)
@@ -488,10 +491,12 @@
 
 def shards(features, hrf_filters, weights, voxel_parcel, parcel_owner):
     owners = lax.axis_size("vox")
+    block = features.shape[0]
     cap = 2 * voxel_parcel.shape[0] // owners
-    place, dest = routes(voxel_parcel, parcel_owner, owners, cap)
-    predicted = predicted_block(features, hrf_filters, weights, lax.axis_size("chan"))
-    packed = packed_slots(predicted, place, dest, owners, cap)
+    sorted_rows, dest = sorted_block(
+        features, hrf_filters, weights, voxel_parcel, parcel_owner, lax.axis_size("chan"), owners
+    )
+    packed = packed_slots(sorted_rows, dest, block, owners, cap)
     return exchange(packed, owners).transpose(0, 2, 1)
 
 

time: 87.3 us -> 83.1 us (0.952)
  Pallas kernels: 82.2 us -> 78.2 us
  local copies, waits for them, and re-layouts: 4.79 us -> 3.78 us
    pallas_call x3 -> x2, Pallas kernels: 59 us -> 55.9 us  [the longest x1 49.3 us: sorted_block(): pl.pallas_call(functools.partial(main_kernel, sizes), out_shape=(jax.Shap...]
    reshape x2 -> x1, local copies, waits for them, and re-layouts: 2.02 us -> 1.3 us  [sorted_block(): jnp.pad(parcel_owner, (0, entries - parcel_owner.shape[0]))]
    unnamed x7 -> x1, local copies, waits for them, and re-layouts: 2.15 us -> 2.49 us
where the time goes in v3:
time: 83.1 us; the launch traced here: 82 us
  Pallas kernels  78.2 us (94%)
  local copies, waits for them, and re-layouts  3.78 us (5%)
    pallas_call x1, Pallas kernels, sorted_block(): pl.pallas_call(functools.partial(main_kernel, sizes), out_shape=(jax.Shap...  49.3 us
    pallas_call x1, Pallas kernels, exchange(): pl.pallas_call(functools.partial(exchange_kernel, n), out_shape=jax.Shape...  22.3 us
    pallas_call x1, Pallas kernels, packed_slots(): pl.pallas_call(functools.partial(pack_kernel, groups, owners, block), out...  6.59 us
    unnamed x1, local copies, waits for them, and re-layouts  2.49 us

profile of v3, /device:TPU:0, one launch (start us, length us, event | category | flops | bytes accessed | tf_op | source)
XLA Modules:
  0.0 82.0 jit_solution(16425335345933240672)
XLA Ops:
  0.0 1.3 %pad_bitcast_fusion.table_ref = s32[13,128]{1,0:T(8,128)} fusion(s32[1600]{0:T(1024)} %param.9), kind=kLoop, calls=%fused_computation | loop fusion | bytes 13056 | tf_op jit(solution)/shard_map/reshape | solution.py:327
  1.3 49.3 %predict.1 = (bf16[9600,128]{1,0:T(8,128)(2,1)}, s32[40,128]{1,0:T(8,128)}) custom-call(bf16[64,5632]{1,0:T(8,128)(2,1)} %feat_ref.1, f32[3,16,704]{2,1,0:T(8,128)} %bitcast.6, bf16[3,704,5120]{2,1,0:T(8,128)(2,1)} %w_ref.1, s32[40,128]{1,0:T(8,128)} %bitcast.7, s32[13,128]{1,0:T(8,128)} %pad_bitcast_fusion.table_ref), custom_call_target="tpu_custom_call" | custom-call | tf_op jit(solution)/shard_map/predict/pallas_call | solution.py:332
  50.6 6.6 %pack.1.in_ref = bf16[16,64,640]{2,1,0:T(8,128)(2,1)} custom-call(s32[40,128]{1,0:T(8,128)} %get-tuple-element.7.dest_ref, bf16[9600,128]{1,0:T(8,128)(2,1)} %get-tuple-element.8.sorted_hbm), custom_call_target="tpu_custom_call" | custom-call | tf_op jit(solution)/shard_map/pack/pallas_call | solution.py:433
  57.2 22.3 %exchange.1 = bf16[16,64,640]{2,1,0:T(8,128)(2,1)} custom-call(bf16[16,64,640]{2,1,0:T(8,128)(2,1)} %pack.1.in_ref), custom_call_target="tpu_custom_call" | custom-call | tf_op jit(solution)/shard_map/exchange/pallas_call | solution.py:479
  79.5 2.5 %copy.7 = bf16[16,640,64]{1,2,0:T(8,128)(2,1)} copy(bf16[16,640,64]{1,2,0:T(8,128)(2,1)} %bitcast.5) | data formatting | bytes 2621440

commit v4 on v3

--- a/solution.py
+++ b/solution.py
@@ -15,7 +15,6 @@
 SORT = 256
 TILE = 8
 LOCAL_TILES = 60
-GROUP = 12
 LAGS = (1, 3, 6, 10)
 
 
@@ -27,14 +26,19 @@
     return jnp.where(mask, 1.0, 0.0).astype(jnp.bfloat16)
 
 
-def route(owners, cap, parcel_ref, table_ref, place_ref, dest_ref):
+def route(owners, cap, parcel_ref, table_ref, place_ref, lists_ref):
     rows = parcel_ref.shape[0]
     parcel = parcel_ref[...]
     high = parcel >> 7
     low = parcel & (LANES - 1)
     owner = jnp.zeros((rows, LANES), jnp.int32)
-    for row in range(table_ref.shape[0]):
-        line = jnp.broadcast_to(table_ref[row : row + 1, :], (rows, LANES))
+    entries = table_ref.shape[0]
+    for row in range(up(entries, LANES) // LANES):
+        line = table_ref[pl.ds(row * LANES, min(LANES, entries - row * LANES))][None, :]
+        if line.shape[1] < LANES:
+            rest = jnp.zeros((1, LANES - line.shape[1]), jnp.int32)
+            line = jnp.concatenate([line, rest], axis=1)
+        line = jnp.broadcast_to(line, (rows, LANES))
         owner = jnp.where(high == row, jnp.take_along_axis(line, low, axis=1), owner)
 
     def iotas(n):
@@ -59,6 +63,7 @@
     first, second = iotas(rows)
     start = dot(ones(second < first), counts).astype(jnp.int32)
     base = dot(ones((second >> 1) < (first >> 1)), counts).astype(jnp.int32)
+    before = dot(ones((second >> 1) < (first >> 1) - 1), counts).astype(jnp.int32)
     count = dot(ones((second >> 1) == (first >> 1)), counts).astype(jnp.int32)
     tile = base >> 3
     tiles = jnp.where(count > 0, ((base & 7) + count + 7) >> 3, 0)
@@ -68,28 +73,46 @@
         return jnp.sum(jnp.where(lane == o, values, 0), axis=1, keepdims=True)
 
     place = jnp.zeros((rows, LANES), jnp.int32)
-    dest = jnp.full((rows, LANES), owners * cap // TILE, jnp.int32)
     offsets = (tile_start - tile) * TILE + start
+    row = lax.broadcasted_iota(jnp.int32, (rows, LANES), 0)
+    whole = (row & 1) == 0
+    empty = rows // 2 * LOCAL_TILES
     for o in range(owners):
         place = jnp.where(owner == o, column(offsets, o) + ranks[o].astype(jnp.int32), place)
-        low_tile = column(tile_start, o)
-        top_tile = low_tile + column(tiles, o)
-        spot = o * (cap // TILE) + column(tile, o) + lane - low_tile
-        dest = jnp.where(jnp.logical_and(lane >= low_tile, lane < top_tile), spot, dest)
+        low = column(tile, o)
+        slot = lane * TILE - column(base, o)
+        opens = jnp.logical_and(whole, jnp.logical_and(slot >= 0, slot < column(count, o)))
+        sources = (row >> 1) * LOCAL_TILES + column(tile_start, o) + lane - low - empty
+
+        def total(mask, values):
+            picked = jnp.where(mask, values.astype(jnp.float32), 0.0)
+            return jnp.sum(picked, axis=0, keepdims=True).astype(jnp.int32)
+
+        single = jnp.ones((rows, LANES), jnp.int32)
+        lists_ref[o : o + 1, :] = jnp.clip(total(opens, sources) + empty, 0, empty)
+        starts = total(jnp.logical_and(whole, low == lane), single)
+        so_far = total(jnp.logical_and(whole, low <= lane), single)
+        so_far = jnp.clip(so_far, 0, rows // 2)
+        lists_ref[owners + o : owners + o + 1, :] = jnp.where(starts > 0, so_far, 0) * owners + o
+    inside = jnp.logical_and((base & 7) != 0, count > 0)
+    added = jnp.where(inside, (row >> 1) * LOCAL_TILES + tile_start, empty)
+    lists_ref[2 * owners : 2 * owners + rows, :] = jnp.clip(added, 0, empty)
+    lists_ref[2 * owners + rows :, :] = jnp.where(tile == before >> 3, 1, 0)
     place_ref[...] = place
-    dest_ref[...] = dest
 
 
 def main_kernel(
     sizes,
-    feat_ref, hrf_ref, w_ref, parcel_ref, table_ref, sorted_ref, dest_ref,
-    wv, fe, series, hrf, coef, design, own, dsend, drecv, rsend, rrecv, place, ordered,
-    w_sem, h_sem, f_local, f_send, f_recv, d_send, d_recv, r_send, r_recv, o_sem,
+    feat_ref, hrf_ref, w_ref, parcel_ref, table_ref, out_ref,
+    wv, fe, series, hrf, coef, design, own, dsend, drecv, rsend, rrecv,
+    place, lists, lists_s, ordered, sums, gathered, packed,
+    w_sem, h_sem, f_local, f_send, f_recv, d_send, d_recv, r_send, r_recv, s_sem, x_local, x_send, x_recv,
 ):
     n_chan, bases, taps, width, wide, block, steps, owners, cap = sizes
     pairs = n_chan // 2
     half = SLAB // 2
     me = lax.axis_index("chan")
+    here = lax.axis_index("vox")
     chip = me // 2
     core = lax.rem(me, 2)
 
@@ -117,7 +140,11 @@
         pl.semaphore_signal(
             barrier, inc=1, device_id={"chan": lax.rem(me + d, n_chan)}, device_id_type=MESH
         )
-    pl.semaphore_wait(barrier, n_chan - 1)
+    for d in range(1, owners):
+        pl.semaphore_signal(
+            barrier, inc=1, device_id={"vox": lax.rem(here + d, owners)}, device_id_type=MESH
+        )
+    pl.semaphore_wait(barrier, n_chan + owners - 2)
 
     parts = [(0, 1, 0, block)]
     parts += [(away, flip, 0, block) for away in (1, 3) for flip in (0, 1)]
@@ -171,7 +198,11 @@
     local.wait()
     widen(me, 0, block)
     arrive(0)
-    route(owners, cap, parcel_ref, table_ref, place, dest_ref)
+    route(owners, cap, parcel_ref, table_ref, place, lists)
+    to_scalars = pltpu.make_async_copy(lists, lists_s, s_sem)
+    to_scalars.start()
+    ordered[ordered.shape[0] - 1] = jnp.zeros((TILE, LANES), jnp.float32)
+    sums[:owners] = jnp.zeros((owners, TILE, LANES), jnp.float32)
 
     span = 32
     spans = block // span
@@ -234,11 +265,6 @@
     local_rows = LOCAL_TILES * TILE
     slab_groups = SLAB // SORT
 
-    def out_copy(i):
-        size = slab_groups * local_rows
-        rows = pl.ds(pl.multiple_of(i * size, 16), size)
-        return pltpu.make_async_copy(ordered.at[rows], sorted_ref.at[rows], o_sem.at[i])
-
     def sort_group(i, k, values):
         group = i * slab_groups + k
         spots = lax.broadcasted_iota(jnp.int32, (local_rows, LANES), 0)
@@ -249,8 +275,13 @@
         rows = lax.dot_general(
             select, twice, (((1,), (1,)), ((), ())), preferred_element_type=jnp.float32
         )
-        here = pl.ds(pl.multiple_of(group * local_rows, 16), local_rows)
-        ordered[here, :] = rows.astype(ordered.dtype)
+        ordered[pl.ds(group * LOCAL_TILES, LOCAL_TILES)] = rows.reshape(LOCAL_TILES, TILE, LANES)
+        added = lists_s.at[pl.ds(2 * owners + 2 * group, 1)]
+        goes_on = lists_s.at[pl.ds(2 * owners + place.shape[0] + 2 * group, 1)]
+        past = sums.at[pl.ds(group * owners, owners)]
+        now = sums.at[pl.ds((group + 1) * owners, owners)]
+        for o in range(owners):
+            now[o] = past[o] * goes_on[0, o].astype(jnp.float32) + ordered[added[0, o]]
 
     def own_part(step, way, i):
         away = pairs - 1 - step if way == 0 else step + 1
@@ -283,8 +314,8 @@
                 ring_copy(step, way, i).start()
             else:
                 sort_group(i, way, total.astype(jnp.bfloat16))
-        if step == pairs - 1:
-            out_copy(i).start()
+
+    to_scalars.wait()
 
     @pl.loop(0, steps + LAGS[-1])
     def _(it):
@@ -300,6 +331,49 @@
                 if step == 0:
                     pair_sum(it - lag)
                 pass_on(step, it - lag)
+
+    side = 4
+    unit = ones(
+        lax.broadcasted_iota(jnp.int32, (block, LANES), 0)
+        == lax.broadcasted_iota(jnp.int32, (block, LANES), 1)
+    )
+
+    def fill(owner):
+        unroll = 8
+        opens = lists_s.at[pl.ds(owner, 1)]
+        rest = lists_s.at[pl.ds(owners + owner, 1)]
+
+        @pl.loop(0, cap // TILE // unroll)
+        def _(s):
+            for u in range(unroll):
+                tile = s * unroll + u
+                gathered[pl.ds(pl.multiple_of(tile * TILE, TILE), TILE), :] = (
+                    ordered[opens[0, tile]] + sums[rest[0, tile]]
+                )
+
+        packed[owner] = lax.dot_general(
+            unit, gathered[...].astype(jnp.bfloat16), (((1,), (1,)), ((), ())),
+            preferred_element_type=jnp.float32,
+        ).astype(packed.dtype)
+
+    def peer_of(d):
+        up_z, up_y = divmod(d, side)
+        return lax.rem(here // side + up_z, owners // side) * side + lax.rem(here + up_y, side)
+
+    def block_copy(d):
+        return pltpu.make_async_remote_copy(
+            src_ref=packed.at[peer_of(d)], dst_ref=out_ref.at[here],
+            send_sem=x_send.at[d - 1], recv_sem=x_recv.at[d - 1],
+            device_id={"vox": peer_of(d)}, device_id_type=MESH,
+        )
+
+    apart = {d: sum(min(k, side - k) for k in divmod(d, side)) for d in range(1, owners)}
+    for d in sorted(apart, key=lambda d: -apart[d]):
+        fill(peer_of(d))
+        block_copy(d).start()
+    fill(here)
+    kept = pltpu.make_async_copy(packed.at[here], out_ref.at[here], x_local)
+    kept.start()
 
     for n in range(len(parts)):
         feature_copy(n).wait_send()
@@ -310,10 +384,13 @@
         for step in range(pairs - 1):
             for way in range(2):
                 ring_copy(step, way, i).wait_send()
-        out_copy(i).wait()
-
-
-def sorted_block(features, hrf_filters, weights, voxel_parcel, parcel_owner, n_chan, owners):
+
+    kept.wait()
+    for d in range(1, owners):
+        block_copy(d).wait()
+
+
+def owned_block(features, hrf_filters, weights, voxel_parcel, parcel_owner, n_chan, owners):
     block, _ = features.shape
     bases, width, taps = hrf_filters.shape
     voxels = weights.shape[2]
@@ -323,20 +400,15 @@
     cap = 2 * voxels // owners
     sizes = (n_chan, bases, taps, width, wide, block, steps, owners, cap)
     parcels = voxel_parcel.reshape(-1, LANES)
-    entries = up(parcel_owner.shape[0], LANES)
-    table = jnp.pad(parcel_owner, (0, entries - parcel_owner.shape[0])).reshape(-1, LANES)
-    sorted_rows = voxels // SORT * LOCAL_TILES * TILE
+    sorted_tiles = voxels // SORT * LOCAL_TILES
     hbm = pl.BlockSpec(memory_space=pl.ANY)
     vmem = pl.BlockSpec(memory_space=pltpu.VMEM)
     dma = pltpu.SemaphoreType.DMA
     return pl.pallas_call(
         functools.partial(main_kernel, sizes),
-        out_shape=(
-            jax.ShapeDtypeStruct((sorted_rows, 2 * block), jnp.bfloat16),
-            jax.ShapeDtypeStruct(parcels.shape, jnp.int32),
-        ),
+        out_shape=jax.ShapeDtypeStruct((owners, block, cap), jnp.bfloat16),
         in_specs=[hbm, hbm, hbm, vmem, vmem],
-        out_specs=(hbm, vmem),
+        out_specs=hbm,
         scratch_shapes=[
             pltpu.VMEM((bases, wide, voxels), jnp.bfloat16),
             pltpu.VMEM((n_chan, block, wide), jnp.bfloat16),
@@ -350,7 +422,12 @@
             pltpu.VMEM((pairs - 1, block, voxels), jnp.bfloat16),
             pltpu.VMEM((pairs - 1, block, voxels), jnp.bfloat16),
             pltpu.VMEM(parcels.shape, jnp.int32),
-            pltpu.VMEM((sorted_rows, 2 * block), jnp.bfloat16),
+            pltpu.VMEM((2 * owners + 2 * parcels.shape[0], LANES), jnp.int32),
+            pltpu.SMEM((2 * owners + 2 * parcels.shape[0], LANES), jnp.int32),
+            pltpu.VMEM((sorted_tiles + 1, TILE, LANES), jnp.float32),
+            pltpu.VMEM(((voxels // SORT + 1) * owners, TILE, LANES), jnp.float32),
+            pltpu.VMEM((cap, LANES), jnp.float32),
+            pltpu.VMEM((owners, block, cap), jnp.bfloat16),
             dma((steps,)),
             dma,
             dma,
@@ -360,144 +437,24 @@
             dma((steps,)),
             dma((pairs - 1, 2, steps)),
             dma((pairs - 1, 2, steps)),
-            dma((steps,)),
+            dma,
+            dma,
+            dma((owners - 1,)),
+            dma((owners - 1,)),
         ],
         compiler_params=pltpu.CompilerParams(
             collective_id=0, has_side_effects=True, vmem_limit_bytes=VMEM_LIMIT
         ),
         name="predict",
-    )(features, hrf_filters.transpose(0, 2, 1), weights, parcels, table)
-
-
-def pack_kernel(groups, owners, block, dest_ref, sorted_hbm, out_ref, held, buf, sem):
-    local_rows = LOCAL_TILES * TILE
-    parts = sem.shape[0]
-    size = groups * local_rows // parts
-
-    def fetch(k):
-        here = pl.ds(k * size, size)
-        return pltpu.make_async_copy(sorted_hbm.at[here], held.at[here], sem.at[k])
-
-    for k in range(parts):
-        fetch(k).start()
-    zero = jnp.zeros((64, LANES), jnp.float32)
-
-    @pl.loop(0, buf.shape[0] // 64)
-    def _(i):
-        buf[pl.ds(pl.multiple_of(i * 64, 64), 64), :] = zero
-
-    for k in range(parts):
-        fetch(k).wait()
-
-        @pl.loop(k * groups // parts, (k + 1) * groups // parts)
-        def _(g):
-            for base in range(0, LOCAL_TILES, GROUP):
-                start = pl.multiple_of(g * local_rows + base * TILE, 2 * TILE)
-                added = held[pl.ds(start, GROUP * TILE), :].astype(jnp.float32)
-                places = [
-                    pl.ds(pl.multiple_of(dest_ref[2 * g, base + n] * TILE, TILE), TILE)
-                    for n in range(GROUP)
-                ]
-                sums = [
-                    buf[spot, :] + added[n * TILE : (n + 1) * TILE]
-                    for n, spot in enumerate(places)
-                ]
-                for spot, value in zip(places, sums):
-                    buf[spot, :] = value
-
-    pairs = owners // 2
-    cap = out_ref.shape[2]
-    left = lax.broadcasted_iota(jnp.int32, (cap, LANES), 1) < block
-    unit = jnp.where(
-        lax.broadcasted_iota(jnp.int32, (LANES, LANES), 0)
-        == lax.broadcasted_iota(jnp.int32, (LANES, LANES), 1),
-        1.0, 0.0,
-    ).astype(jnp.bfloat16)
-
-    @pl.loop(0, pairs)
-    def _(p):
-        first = buf[pl.ds(pl.multiple_of(p * cap, LANES), cap), :]
-        second = buf[pl.ds(pl.multiple_of((pairs + p) * cap, LANES), cap), :]
-        both = jnp.where(left, first, second).astype(jnp.bfloat16)
-        turned = lax.dot_general(
-            unit, both, (((1,), (1,)), ((), ())), preferred_element_type=jnp.float32
-        ).astype(out_ref.dtype)
-        out_ref[p] = turned[:block]
-        out_ref[pairs + p] = turned[block:]
-
-
-def packed_slots(sorted_rows, dest, block, owners, cap):
-    rows = sorted_rows.shape[0]
-    groups = rows // (LOCAL_TILES * TILE)
-    hbm = pl.BlockSpec(memory_space=pl.ANY)
-    return pl.pallas_call(
-        functools.partial(pack_kernel, groups, owners, block),
-        out_shape=jax.ShapeDtypeStruct((owners, block, cap), jnp.bfloat16),
-        in_specs=[pl.BlockSpec(memory_space=pltpu.SMEM), hbm],
-        out_specs=pl.BlockSpec(memory_space=pltpu.VMEM),
-        scratch_shapes=[
-            pltpu.VMEM(sorted_rows.shape, sorted_rows.dtype),
-            pltpu.VMEM((owners * cap + 64, LANES), jnp.float32),
-            pltpu.SemaphoreType.DMA((4,)),
-        ],
-        compiler_params=pltpu.CompilerParams(vmem_limit_bytes=60_000_000),
-        name="pack",
-    )(dest, sorted_rows)
-
-
-def exchange_kernel(n, in_ref, out_ref, local_sem, send_sem, recv_sem):
-    me = lax.axis_index("vox")
-    side = 4
-    local = pltpu.make_async_copy(in_ref.at[me], out_ref.at[me], local_sem)
-    local.start()
-    barrier = pltpu.get_barrier_semaphore()
-    for d in range(1, n):
-        pl.semaphore_signal(
-            barrier, inc=1, device_id={"vox": lax.rem(me + d, n)}, device_id_type=MESH
-        )
-    pl.semaphore_wait(barrier, n - 1)
-
-    def block_copy(d):
-        up_z, up_y = divmod(d, side)
-        peer = lax.rem(me // side + up_z, n // side) * side + lax.rem(me + up_y, side)
-        return pltpu.make_async_remote_copy(
-            src_ref=in_ref.at[peer], dst_ref=out_ref.at[me],
-            send_sem=send_sem.at[d - 1], recv_sem=recv_sem.at[d - 1],
-            device_id={"vox": peer}, device_id_type=MESH,
-        )
-
-    apart = {d: sum(min(k, side - k) for k in divmod(d, side)) for d in range(1, n)}
-    for d in sorted(apart, key=lambda d: -apart[d]):
-        block_copy(d).start()
-    local.wait()
-    for d in range(1, n):
-        block_copy(d).wait()
-
-
-def exchange(packed, n):
-    dma = pltpu.SemaphoreType.DMA
-    return pl.pallas_call(
-        functools.partial(exchange_kernel, n),
-        out_shape=jax.ShapeDtypeStruct(packed.shape, packed.dtype),
-        in_specs=[pl.BlockSpec(memory_space=pl.ANY)],
-        out_specs=pl.BlockSpec(memory_space=pl.ANY),
-        scratch_shapes=[dma, dma((n - 1,)), dma((n - 1,))],
-        compiler_params=pltpu.CompilerParams(
-            collective_id=1, has_side_effects=True, vmem_limit_bytes=60_000_000
-        ),
-        name="exchange",
-    )(packed)
+    )(features, hrf_filters.transpose(0, 2, 1), weights, parcels, parcel_owner)
 
 
 def shards(features, hrf_filters, weights, voxel_parcel, parcel_owner):
     owners = lax.axis_size("vox")
-    block = features.shape[0]
-    cap = 2 * voxel_parcel.shape[0] // owners
-    sorted_rows, dest = sorted_block(
+    owned = owned_block(
         features, hrf_filters, weights, voxel_parcel, parcel_owner, lax.axis_size("chan"), owners
     )
-    packed = packed_slots(sorted_rows, dest, block, owners, cap)
-    return exchange(packed, owners).transpose(0, 2, 1)
+    return owned.transpose(0, 2, 1)
 
 
 def solution(mesh):

time: 83.1 us -> 73.7 us (0.89)
  Pallas kernels: 78.2 us -> 70.1 us
  local copies, waits for them, and re-layouts: 3.78 us -> 2.49 us
    pallas_call x3 -> x1, Pallas kernels: 78.2 us -> 70.1 us  [owned_block(): pl.pallas_call(functools.partial(main_kernel, sizes), out_shape=jax.Shape...]
    reshape x1 -> x0, local copies, waits for them, and re-layouts: 1.3 us -> none  [sorted_block(): jnp.pad(parcel_owner, (0, entries - parcel_owner.shape[0]))]
where the time goes in v4:
time: 73.7 us; the launch traced here: 72.6 us
  Pallas kernels  70.1 us (95%)
  local copies, waits for them, and re-layouts  2.49 us (3%)
    pallas_call x1, Pallas kernels, owned_block(): pl.pallas_call(functools.partial(main_kernel, sizes), out_shape=jax.Shape...  70.1 us
    unnamed x1, local copies, waits for them, and re-layouts  2.49 us

profile of v4, /device:TPU:0, one launch (start us, length us, event | category | flops | bytes accessed | tf_op | source)
XLA Modules:
  0.0 72.6 jit_solution(16147482103062472094)
XLA Ops:
  0.0 70.1 %predict.1 = bf16[16,64,640]{2,1,0:T(8,128)(2,1)} custom-call(bf16[64,5632]{1,0:T(8,128)(2,1)} %feat_ref.1, f32[3,16,704]{2,1,0:T(8,128)} %bitcast.4, bf16[3,704,5120]{2,1,0:T(8,128)(2,1)} %w_ref.1, s32[40,128]{1,0:T(8,128)} %bitcast.5, s32[1600]{0:T(1024)} %table_ref.1), custom_call_target="tpu_custom_call" | custom-call | tf_op jit(solution)/shard_map/predict/pallas_call | solution.py:407
  70.1 2.5 %copy.7 = bf16[16,640,64]{1,2,0:T(8,128)(2,1)} copy(bf16[16,640,64]{1,2,0:T(8,128)(2,1)} %bitcast.3) | data formatting | bytes 2621440

commit v5 on v4

--- a/solution.py
+++ b/solution.py
@@ -9,7 +9,7 @@
 
 MESH = pl.DeviceIdType.MESH
 TAP_SPACING = 2
-VMEM_LIMIT = 66_000_000
+VMEM_LIMIT = 60_000_000
 LANES = 128
 SLAB = 512
 SORT = 256
@@ -406,7 +406,7 @@
     dma = pltpu.SemaphoreType.DMA
     return pl.pallas_call(
         functools.partial(main_kernel, sizes),
-        out_shape=jax.ShapeDtypeStruct((owners, block, cap), jnp.bfloat16),
+        out_shape=pltpu.VMEM((owners, block, cap), jnp.bfloat16),
         in_specs=[hbm, hbm, hbm, vmem, vmem],
         out_specs=hbm,
         scratch_shapes=[

time: 73.7 us -> 72.2 us (0.980)
  local copies, waits for them, and re-layouts: 2.49 us -> 1.06 us
    unnamed x1, local copies, waits for them, and re-layouts: 2.49 us -> 1.06 us
where the time goes in v5:
time: 72.2 us; the launch traced here: 71.1 us
  Pallas kernels  70 us (97%)
  local copies, waits for them, and re-layouts  1.06 us (1%)
    pallas_call x1, Pallas kernels, owned_block(): pl.pallas_call(functools.partial(main_kernel, sizes), out_shape=pltpu.VME...  70 us

profile of v5, /device:TPU:0, one launch (start us, length us, event | category | flops | bytes accessed | tf_op | source)
XLA Modules:
  0.0 71.1 jit_solution(8395095064941026326)
XLA Ops:
  0.0 70.0 %predict.1 = bf16[16,64,640]{2,1,0:T(8,128)(2,1)S(1)} custom-call(bf16[64,5632]{1,0:T(8,128)(2,1)} %feat_ref.1, f32[3,16,704]{2,1,0:T(8,128)} %bitcast.4, bf16[3,704,5120]{2,1,0:T(8,128)(2,1)} %w_ref.1, s32[40,128]{1,0:T(8,128)} %bitcast.5, s32[1600]{0:T(1024)} %table_ref.1), custom_call_target="tpu_custom_call" | custom-call | tf_op jit(solution)/shard_map/predict/pallas_call | solution.py:407
  70.0 1.1 %copy.7 = bf16[16,640,64]{1,2,0:T(8,128)(2,1)} copy(bf16[16,640,64]{1,2,0:T(8,128)(2,1)S(1)} %bitcast.3) | data formatting | bytes 2621440
